TPU v7x, 32 devices: a whole 2x2x4 slice. The times are simulated.
32 devices in a mesh: seq: 8 (over z, x), batch: 4 (over y, core).
Axes of the slice: x: 2, y: 2, z: 4, core: 2. Of those that a mesh axis runs over, the one named last changes fastest.
Arguments:
- hidden: bfloat16 [8, 2048, 4096], P('batch', None, 'seq')
- gain: float32 [4096], P('seq'), may hold values from 0.5 to 1.5
- value_weight: float32 [4096], P('seq'), may hold values from -0.09375 to 0.09375
- rewards: float32 [8, 2048], P('batch', 'seq'), may hold values from -1.5 to 1.5
- reward_mask: int32 [8, 2048], P('batch', 'seq'), may hold values 0 or 1
- lengths: int32 [8], P('batch'), may hold values from 512 to 2048
- horizon: float32 [8], P('batch'), may hold values from 24 to 16384
Outputs:
- advantages: float32 [8, 2048], P(None, ('seq', 'batch'))
- returns: float32 [8, 2048], P(None, ('seq', 'batch'))
All inputs are finite; a program needn't handle non-finite values. No bound on the sum of `reward_mask` on one device may be relied on, other than what follows from the above.
Results may differ from a plain program's by a relative error of at most 0.0003.
Values may be sent and summed in bfloat16 or wider, within the bound.
A program may use at most 64 MiB of HBM per device.

v0:
```python
import functools

import jax
import jax.numpy as jnp
from jax import lax
from jax.experimental import pallas as pl
from jax.experimental.pallas import tpu as pltpu
from jax.sharding import PartitionSpec as P

EPS = 1e-05
LANES = 128
F32 = jnp.float32


def kernel(n, nb, owners, hidden, gain, weight, rewards, mask, lengths, horizon,
           out_ref,
           hv, gain_v, weight_v, rew_v, mask_v, len_s, hor_s,
           part, rbuf, rw_send, rw_recv, len_send, len_recv, hor_send, hor_recv,
           sum_send, sum_recv, tok_send, tok_recv,
           chunk_sem, small_sem, part_ss, part_rs, rw_ss, rw_rs, info_ss, info_rs,
           sum_ss, sum_rs, tok_ss, tok_rs):
    R, T, depth = hidden.shape
    block = rewards.shape[1]
    width = block // nb
    per = n // owners
    base = (n - owners) // 2
    L = T // owners
    G = L // LANES
    gb = block // LANES
    rows = G * R
    total = depth * n
    s = lax.axis_index("seq")
    b = lax.axis_index("batch")
    is_owner = (s >= base) & (s < base + owners)
    mine = s - base
    out_o = s // per
    rw_at = base + out_o
    half = s % per

    def chunk_copy(o, r):
        span = pl.ds(o * L, L)
        return pltpu.make_async_copy(hidden.at[r, span, :], hv.at[r, span, :], chunk_sem.at[o, r])

    smalls = [
        pltpu.make_async_copy(src, dst, small_sem.at[i])
        for i, (src, dst) in enumerate(
            ((gain, gain_v), (weight, weight_v), (rewards, rew_v), (mask, mask_v),
             (lengths, len_s), (horizon, hor_s)))
    ]
    for copy in smalls:
        copy.start()
    near_high = s * (owners // 2) // n
    near_low = s % 2

    def turn(k):
        back = owners - 1 - k
        if owners % 2:
            return (s + back) % owners
        return (near_high + back // 2) % (owners // 2) * 2 + (near_low + back) % 2

    for k in range(owners):
        for r in range(R):
            chunk_copy(turn(k), r).start()
    barrier = pltpu.get_barrier_semaphore()
    for k in range(1, n):
        peer = (s + k) % n

        @pl.when(is_owner | ((peer >= base) & (peer < base + owners)))
        def _():
            pl.semaphore_signal(barrier, inc=1, device_id={"seq": peer},
                                device_id_type=pl.DeviceIdType.MESH)
    for k in range(1, nb):
        pl.semaphore_signal(barrier, inc=1, device_id={"batch": lax.rem(b + k, nb)},
                            device_id_type=pl.DeviceIdType.MESH)
    for copy in smalls:
        copy.wait()

    head = (gain_v[...] * weight_v[...]).reshape(1, depth)
    high = head.astype(jnp.bfloat16).astype(F32)
    middle = (head - high).astype(jnp.bfloat16).astype(F32)
    low = head - high - middle
    wrow = lax.broadcasted_iota(jnp.int32, (16, depth), 0)
    pieces = jnp.where(wrow == 0, high, jnp.where(wrow == 1, middle, jnp.where(wrow == 2, low, 0.0)))
    pieces = pieces.astype(jnp.bfloat16)

    rw = rew_v[...] * mask_v[...].astype(F32)
    for g in range(gb):
        rw_send[g * R:(g + 1) * R, :] = rw[:, g * LANES:(g + 1) * LANES]
    for r in range(R):
        len_send[r:r + 1, :] = jnp.full((1, LANES), len_s[r], jnp.int32)
        hor_send[r:r + 1, :] = jnp.full((1, LANES), hor_s[r], F32)

    infos = []
    for k in range(1, nb):
        for i, (src, dst) in enumerate(((len_send, len_recv), (hor_send, hor_recv))):
            infos.append((k, i, src, dst))

    def info_copy(k, i, src, dst):
        return pltpu.make_async_remote_copy(
            src, dst.at[b], info_ss.at[i, k], info_rs.at[i, b],
            device_id={"batch": lax.rem(b + k, nb)}, device_id_type=pl.DeviceIdType.MESH)

    def info_arrived(k, i, src, dst):
        at = lax.rem(b + k, nb)
        return pltpu.make_async_remote_copy(
            src, dst.at[at], info_ss.at[i, k], info_rs.at[i, at],
            device_id={"batch": at}, device_id_type=pl.DeviceIdType.MESH)

    def part_copy(o):
        return pltpu.make_async_remote_copy(
            part.at[o], rbuf.at[s], part_ss.at[o], part_rs.at[s],
            device_id={"seq": base + o}, device_id_type=pl.DeviceIdType.MESH)

    def rw_copy():
        return pltpu.make_async_remote_copy(
            rw_send, rw_recv.at[half], rw_ss, rw_rs.at[half],
            device_id={"seq": rw_at}, device_id_type=pl.DeviceIdType.MESH)

    def send_part(o):
        @pl.when(base + o != s)
        def _():
            part_copy(o).start()

    meet = min(1, owners - 1)

    def compute(k, carry):
        o = turn(k)
        for r in range(R):
            chunk_copy(o, r).wait()
            for g in range(G):
                at = pl.ds(pl.multiple_of(o * L + g * LANES, LANES), LANES)
                h = hv[r, at, :]
                sums = lax.dot_general(pieces, h, (((1,), (1,)), ((), ())),
                                       preferred_element_type=F32)
                squares = jnp.zeros((LANES, LANES), F32)
                for j in range(depth // LANES):
                    wide = h[:, j * LANES:(j + 1) * LANES].astype(F32)
                    squares = squares + wide * wide
                row = g * R + r
                part[o, 0, row:row + 1, :] = jnp.sum(sums[0:8], 0, keepdims=True)
                part[o, 1, row:row + 1, :] = jnp.sum(squares.T, 0, keepdims=True)

        @pl.when(k == meet)
        def _():
            met = jnp.where(is_owner, n - 1, owners) + nb - 1
            pl.semaphore_wait(barrier, met)
            for before in range(meet):
                send_part(turn(before))

            @pl.when(rw_at != s)
            def _():
                rw_copy().start()

            for entry in infos:
                info_copy(*entry).start()

        @pl.when(k >= meet)
        def _():
            send_part(o)
        return carry

    lax.fori_loop(0, owners, compute, 0)

    @pl.when(rw_at == s)
    def _():
        rw_recv[half] = rw_send[...]

    len_recv[b] = len_send[...]
    hor_recv[b] = hor_send[...]

    def sum_copy(i, j):
        return pltpu.make_async_remote_copy(
            sum_send, sum_recv.at[mine, b], sum_ss.at[i, j], sum_rs.at[mine, b],
            device_id={"seq": i, "batch": j}, device_id_type=pl.DeviceIdType.MESH)

    def each_sum(act):
        def one(i):
            for j in range(nb):
                if isinstance(i, int) and not base <= i < base + owners:
                    act(sum_copy(i, j))
                else:
                    @pl.when((i != s) | (j != b))
                    def _():
                        act(sum_copy(i, j))

        if n * nb <= 32:
            for i in range(n):
                one(i)
        else:
            def body(i, carry):
                one(i)
                return carry
            lax.fori_loop(0, n, body, 0)

    def tok_copy(h, j):
        c = lax.rem(b + j, nb)
        g = h * gb + (c * width) // LANES
        return pltpu.make_async_remote_copy(
            tok_send.at[g], tok_recv.at[b], tok_ss.at[h, j], tok_rs.at[b],
            device_id={"seq": mine * per + h, "batch": c}, device_id_type=pl.DeviceIdType.MESH)

    def tok_local(h):
        g = h * gb + (b * width) // LANES
        return pltpu.make_async_copy(tok_send.at[g], tok_recv.at[b], tok_rs.at[b])

    @pl.when(is_owner)
    def _():
        row = lax.broadcasted_iota(jnp.int32, (rows, LANES), 0)
        lane = lax.broadcasted_iota(jnp.int32, (rows, LANES), 1)
        group = row // R
        which = row % R
        length = jnp.full((rows, LANES), len_s[0], jnp.int32)
        reach = jnp.full((rows, LANES), hor_s[0], F32)
        for r in range(1, R):
            length = jnp.where(which == r, len_s[r], length)
            reach = jnp.where(which == r, hor_s[r], reach)
        rate = -1.0 / reach
        local = group * LANES + lane
        token = mine * L + local
        valid = (token < length).astype(F32)
        next_valid = (token + 1 < length).astype(F32)
        levels = [[j * k for j in range(1, min(8, LANES // k))] for k in (1, 8, 64)]
        lane_decay = [[jnp.where(lane < LANES - k, jnp.exp(rate * k), 0.0) for k in level]
                      for level in levels]
        hops = [1 << i for i in range(max(G - 1, 0).bit_length())]
        row_decay = [jnp.where(group + k < G, jnp.exp(rate * (k * LANES)), 0.0) for k in hops]
        into = jnp.where(group < G - 1, jnp.exp(rate * (LANES - lane).astype(F32)), 0.0)
        power = jnp.exp(rate * (L - 1 - local).astype(F32))
        decay = jnp.exp(rate)
        power_sum = jnp.sum(power, 1, keepdims=True)
        power_squares = jnp.sum(power * power, 1, keepdims=True)

        for h in range(per):
            @pl.when(mine * per + h != s)
            def _():
                pltpu.make_async_remote_copy(
                    rw_send, rw_recv.at[h], rw_ss, rw_rs.at[h],
                    device_id={"seq": s}, device_id_type=pl.DeviceIdType.MESH).wait_recv()
        gains = jnp.concatenate([rw_recv[h] for h in range(per)], 0)

        rbuf[s] = part[mine]
        for k in range(1, n):
            at = (s + k) % n
            pltpu.make_async_remote_copy(
                part.at[0], rbuf.at[at], part_ss.at[0], part_rs.at[at],
                device_id={"seq": at}, device_id_type=pl.DeviceIdType.MESH).wait_recv()
        projected = rbuf[0, 0]
        squares = rbuf[0, 1]
        for k in range(1, n):
            projected = projected + rbuf[k, 0]
            squares = squares + rbuf[k, 1]
        values = projected * lax.rsqrt(squares / total + EPS)
        ahead = pltpu.roll(values, LANES - 1, 1)
        if G > 1:
            after = jnp.where(group < G - 1, pltpu.roll(ahead, rows - R, 0), 0.0)
        else:
            after = jnp.zeros_like(ahead)
        next_values = jnp.where(lane == LANES - 1, after, ahead)
        gae = (gains + next_valid * next_values - values) * valid
        for level, factors in zip(levels, lane_decay):
            terms = [factor * pltpu.roll(gae, LANES - k, 1) for k, factor in zip(level, factors)]
            gae = gae + sum(terms[1:], terms[0])
        if G > 1:
            start = jnp.broadcast_to(gae[:, 0:1], (rows, LANES))
            for k, factor in zip(hops, row_decay):
                start = start + factor * pltpu.roll(start, rows - k * R, 0)
            gae = gae + into * pltpu.roll(start, rows - R, 0)
        for g in range(G):
            tok_send[g, 0] = gae[g * R:(g + 1) * R]
            tok_send[g, 1] = values[g * R:(g + 1) * R]
        sums = jnp.where(lane == 1, jnp.sum(gae, 1, keepdims=True), 0.0)
        sums = jnp.where(lane == 2, 2.0 * jnp.sum(gae * power, 1, keepdims=True), sums)
        sums = jnp.where(lane == 3, jnp.sum(gae * gae, 1, keepdims=True), sums)
        sums = jnp.where(lane == 4, power_sum, sums)
        sums = jnp.where(lane == 5, power_squares, sums)
        sums = jnp.where((lane == 0) & (group == 0), values + decay * gae, sums)
        summary = sums[0:R]
        for g in range(1, G):
            summary = summary + sums[g * R:(g + 1) * R]
        sum_send[...] = summary
        pltpu.make_async_copy(sum_send, sum_recv.at[mine, b], sum_rs.at[mine, b]).start()
        each_sum(lambda copy: copy.start())
        for h in range(per):
            for j in range(1, nb):
                tok_copy(h, j).start()

            @pl.when(mine * per + h == s)
            def _():
                tok_local(h).start()

            @pl.when(mine * per + h != s)
            def _():
                tok_copy(h, 0).start()

    for o in range(owners):
        @pl.when(base + o != s)
        def _():
            part_copy(o).wait_send()

    @pl.when(rw_at != s)
    def _():
        rw_copy().wait_send()

    for entry in infos:
        info_copy(*entry).wait_send()

    for entry in infos:
        info_arrived(*entry).wait_recv()
    lane = lax.broadcasted_iota(jnp.int32, (R, LANES), 1)
    group_out = half * gb + (b * width) // LANES
    local = group_out * LANES + lane
    token = out_o * L + local
    count = jnp.zeros((R, LANES), F32)
    jump, power_out, valid_out, lens = [], [], [], []
    for c in range(nb):
        length = len_recv[c]
        rate = -1.0 / hor_recv[c]
        count = count + jnp.minimum(length, T).astype(F32)
        jump.append(jnp.exp(rate * float(L)))
        power_out.append(jnp.exp(rate * (L - 1 - local).astype(F32)))
        valid_out.append((token < length).astype(F32))
        lens.append(length)
    count = jnp.sum(count, 0, keepdims=True)

    @pl.when(is_owner)
    def _():
        each_sum(lambda copy: copy.wait_send())
        for h in range(per):
            for j in range(1, nb):
                tok_copy(h, j).wait_send()

            @pl.when(mine * per + h != s)
            def _():
                tok_copy(h, 0).wait_send()

    for o in range(owners):
        for c in range(nb):
            pltpu.make_async_remote_copy(
                sum_send, sum_recv.at[o, c], sum_ss.at[0, 0], sum_rs.at[o, c],
                device_id={"seq": base + o, "batch": c},
                device_id_type=pl.DeviceIdType.MESH).wait_recv()

    acc = jnp.zeros((R, LANES), F32)
    entering = []
    for c in range(nb):
        u = jnp.zeros((R, LANES), F32)
        chosen = jnp.zeros((R, LANES), F32)
        for o in reversed(range(owners)):
            message = sum_recv[o, c]
            factor = jnp.where((lane == 1) | (lane == 3), 1.0,
                               jnp.where((lane == 2) | (lane == 4), u,
                                         jnp.where(lane == 5, u * u, 0.0)))
            acc = acc + message * factor
            chosen = jnp.where(out_o == o, u, chosen)
            if o:
                first_value = jnp.broadcast_to(message[:, 0:1], (R, LANES))
                u = jnp.where(o * L < lens[c], first_value + jump[c] * u, 0.0)
        entering.append(chosen)
    acc = jnp.sum(acc, 0, keepdims=True)
    lane1 = lax.broadcasted_iota(jnp.int32, (1, LANES), 1)
    first = jnp.sum(jnp.where((lane1 == 1) | (lane1 == 4), acc, 0.0), 1, keepdims=True)
    second = jnp.sum(jnp.where((lane1 == 2) | (lane1 == 3) | (lane1 == 5), acc, 0.0), 1, keepdims=True)
    mean = first / count
    var = jnp.maximum(second / count - mean * mean, 1.0)
    scale = lax.rsqrt(var)

    for c in range(nb):
        pltpu.make_async_remote_copy(
            tok_send.at[0], tok_recv.at[c], tok_ss.at[0, 0], tok_rs.at[c],
            device_id={"seq": rw_at, "batch": c},
            device_id_type=pl.DeviceIdType.MESH).wait_recv()
    spots = LANES // width
    spot = b % spots

    def pick(x):
        result = x[:, 0:width]
        for j in range(1, spots):
            result = jnp.where(spot == j, x[:, j * width:(j + 1) * width], result)
        return result

    for c in range(nb):
        gae = tok_recv[c, 0] + power_out[c] * entering[c]
        out_ref[(nb + c) * R:(nb + c + 1) * R, :] = pick((gae + tok_recv[c, 1]) * valid_out[c])
        out_ref[c * R:(c + 1) * R, :] = pick((gae - mean) * valid_out[c] * scale)


def per_device(hidden, gain, weight, rewards, mask, lengths, horizon):
    n = lax.axis_size("seq")
    nb = lax.axis_size("batch")
    owners = n // 2 if n % 4 == 0 else n
    R, T, depth = hidden.shape
    block = rewards.shape[1]
    per = n // owners
    G = T // owners // LANES
    gb = block // LANES
    rows = G * R
    dma = pltpu.SemaphoreType.DMA
    both = pl.pallas_call(
        functools.partial(kernel, n, nb, owners),
        out_shape=pltpu.VMEM((2 * R * nb, block // nb), F32),
        in_specs=[pl.BlockSpec(memory_space=pl.ANY)] * 7,
        out_specs=pl.BlockSpec(memory_space=pltpu.VMEM),
        scratch_shapes=[
            pltpu.VMEM((R, T, depth), jnp.bfloat16),
            pltpu.VMEM((depth,), F32),
            pltpu.VMEM((depth,), F32),
            pltpu.VMEM((R, block), F32),
            pltpu.VMEM((R, block), jnp.int32),
            pltpu.SMEM((R,), jnp.int32),
            pltpu.SMEM((R,), F32),
            pltpu.VMEM((owners, 2, rows, LANES), F32),
            pltpu.VMEM((n, 2, rows, LANES), F32),
            pltpu.VMEM((gb * R, LANES), F32),
            pltpu.VMEM((per, gb * R, LANES), F32),
            pltpu.VMEM((R, LANES), jnp.int32),
            pltpu.VMEM((nb, R, LANES), jnp.int32),
            pltpu.VMEM((R, LANES), F32),
            pltpu.VMEM((nb, R, LANES), F32),
            pltpu.VMEM((R, LANES), F32),
            pltpu.VMEM((owners, nb, R, LANES), F32),
            pltpu.VMEM((G, 2, R, LANES), F32),
            pltpu.VMEM((nb, 2, R, LANES), F32),
            dma((owners, R)), dma((6,)),
            dma((owners,)), dma((n,)),
            dma(()), dma((per,)),
            dma((2, nb)), dma((2, nb)),
            dma((n, nb)), dma((owners, nb)),
            dma((per, nb)), dma((nb,)),
        ],
        compiler_params=pltpu.CompilerParams(collective_id=0, has_side_effects=True),
    )(hidden, gain, weight, rewards, mask, lengths, horizon)
    return both[:R * nb], both[R * nb:]


def solution(mesh):
    return jax.shard_map(
        per_device,
        mesh=mesh,
        in_specs=(
            P("batch", None, "seq"),
            P("seq"),
            P("seq"),
            P("batch", "seq"),
            P("batch", "seq"),
            P("batch"),
            P("batch"),
        ),
        out_specs=(P(None, ("seq", "batch")), P(None, ("seq", "batch"))),
        check_vma=False,
    )
```

profile of v0, /device:TPU:0, one launch (start us, length us, event | category | flops | bytes accessed | tf_op | source)
XLA Modules:
  0.0 17.3 jit_solution(512348994866865005)
XLA Ops:
  0.6 16.1 %shard_map.86 = f32[16,64]{1,0:T(8,128)S(1)} custom-call(bf16[2,2048,512]{2,1,0:T(8,128)(2,1)} %hidden.1, f32[512]{0:T(512)} %gain.1, f32[512]{0:T(512)} %weight.1, f32[2,256]{1,0:T(2,128)} %rewards.1, s32[2,256]{1,0:T(2,128)} %mask.1, s32[2]{0:T(128)} %lengths.1, f32[2]{0:T(128)} %horizon.1), custom_call_target="tpu_custom_call" | custom-call | tf_op jit(solution)/shard_map/pallas_call | solution.py:398
  16.7 0.6 %fusion = (f32[8,64]{1,0:T(8,128)}, f32[8,64]{1,0:T(8,128)}) fusion(f32[16,64]{1,0:T(8,128)S(1)} %shard_map.86), kind=kLoop, calls=%fused_computation | loop fusion | bytes 8192 | tf_op jit(solution)/shard_map/slice | solution.py:432
where the time goes:
time: 17.5 us; the launch traced here: 17.3 us
  Pallas kernels  16.1 us (92%)
  between operations  0.64 us (4%)
  local copies, waits for them, and re-layouts  0.6 us (3%)
    pallas_call x1, Pallas kernels, per_device(): pl.pallas_call(functools.partial(kernel, n, nb, owners), out_shape=pltpu....  16.1 us
    slice x1, local copies, waits for them, and re-layouts, per_device(): return (both[:R * nb], both[R * nb:])  0.6 us

commit v1 on v0

--- a/solution.py
+++ b/solution.py
@@ -18,7 +18,7 @@
            part, rbuf, rw_send, rw_recv, len_send, len_recv, hor_send, hor_recv,
            sum_send, sum_recv, tok_send, tok_recv,
            chunk_sem, small_sem, part_ss, part_rs, rw_ss, rw_rs, info_ss, info_rs,
-           sum_ss, sum_rs, tok_ss, tok_rs):
+           sum_ss, sum_rs, tok_ss, tok_rs, sum_all, tok_all):
     R, T, depth = hidden.shape
     block = rewards.shape[1]
     width = block // nb
@@ -97,23 +97,20 @@
 
     def info_copy(k, i, src, dst):
         return pltpu.make_async_remote_copy(
-            src, dst.at[b], info_ss.at[i, k], info_rs.at[i, b],
+            src, dst.at[b], info_ss.at[i], info_rs.at[i],
             device_id={"batch": lax.rem(b + k, nb)}, device_id_type=pl.DeviceIdType.MESH)
 
-    def info_arrived(k, i, src, dst):
-        at = lax.rem(b + k, nb)
-        return pltpu.make_async_remote_copy(
-            src, dst.at[at], info_ss.at[i, k], info_rs.at[i, at],
-            device_id={"batch": at}, device_id_type=pl.DeviceIdType.MESH)
+    def bytes_of(ref, sem):
+        return pltpu.make_async_copy(ref, ref, sem)
 
     def part_copy(o):
         return pltpu.make_async_remote_copy(
-            part.at[o], rbuf.at[s], part_ss.at[o], part_rs.at[s],
+            part.at[o], rbuf.at[s], part_ss, part_rs,
             device_id={"seq": base + o}, device_id_type=pl.DeviceIdType.MESH)
 
     def rw_copy():
         return pltpu.make_async_remote_copy(
-            rw_send, rw_recv.at[half], rw_ss, rw_rs.at[half],
+            rw_send, rw_recv.at[half], rw_ss, rw_rs,
             device_id={"seq": rw_at}, device_id_type=pl.DeviceIdType.MESH)
 
     def send_part(o):
@@ -170,7 +167,7 @@
 
     def sum_copy(i, j):
         return pltpu.make_async_remote_copy(
-            sum_send, sum_recv.at[mine, b], sum_ss.at[i, j], sum_rs.at[mine, b],
+            sum_send, sum_recv.at[mine, b], sum_ss, sum_rs,
             device_id={"seq": i, "batch": j}, device_id_type=pl.DeviceIdType.MESH)
 
     def each_sum(act):
@@ -196,12 +193,12 @@
         c = lax.rem(b + j, nb)
         g = h * gb + (c * width) // LANES
         return pltpu.make_async_remote_copy(
-            tok_send.at[g], tok_recv.at[b], tok_ss.at[h, j], tok_rs.at[b],
+            tok_send.at[g], tok_recv.at[b], tok_ss, tok_rs,
             device_id={"seq": mine * per + h, "batch": c}, device_id_type=pl.DeviceIdType.MESH)
 
     def tok_local(h):
         g = h * gb + (b * width) // LANES
-        return pltpu.make_async_copy(tok_send.at[g], tok_recv.at[b], tok_rs.at[b])
+        tok_recv[b] = tok_send[g]
 
     @pl.when(is_owner)
     def _():
@@ -230,20 +227,18 @@
         power_sum = jnp.sum(power, 1, keepdims=True)
         power_squares = jnp.sum(power * power, 1, keepdims=True)
 
-        for h in range(per):
-            @pl.when(mine * per + h != s)
-            def _():
-                pltpu.make_async_remote_copy(
-                    rw_send, rw_recv.at[h], rw_ss, rw_rs.at[h],
-                    device_id={"seq": s}, device_id_type=pl.DeviceIdType.MESH).wait_recv()
+        @pl.when(s // per == mine)
+        def _():
+            if per > 1:
+                bytes_of(rw_recv.at[pl.ds(0, per - 1)], rw_rs).wait()
+
+        @pl.when(s // per != mine)
+        def _():
+            bytes_of(rw_recv, rw_rs).wait()
         gains = jnp.concatenate([rw_recv[h] for h in range(per)], 0)
 
         rbuf[s] = part[mine]
-        for k in range(1, n):
-            at = (s + k) % n
-            pltpu.make_async_remote_copy(
-                part.at[0], rbuf.at[at], part_ss.at[0], part_rs.at[at],
-                device_id={"seq": at}, device_id_type=pl.DeviceIdType.MESH).wait_recv()
+        bytes_of(rbuf.at[pl.ds(0, n - 1)], part_rs).wait()
         projected = rbuf[0, 0]
         squares = rbuf[0, 1]
         for k in range(1, n):
@@ -278,7 +273,7 @@
         for g in range(1, G):
             summary = summary + sums[g * R:(g + 1) * R]
         sum_send[...] = summary
-        pltpu.make_async_copy(sum_send, sum_recv.at[mine, b], sum_rs.at[mine, b]).start()
+        sum_recv[mine, b] = summary
         each_sum(lambda copy: copy.start())
         for h in range(per):
             for j in range(1, nb):
@@ -286,26 +281,27 @@
 
             @pl.when(mine * per + h == s)
             def _():
-                tok_local(h).start()
+                tok_local(h)
 
             @pl.when(mine * per + h != s)
             def _():
                 tok_copy(h, 0).start()
 
-    for o in range(owners):
-        @pl.when(base + o != s)
-        def _():
-            part_copy(o).wait_send()
+    @pl.when(is_owner)
+    def _():
+        bytes_of(part.at[pl.ds(0, owners - 1)], part_ss).wait()
+
+    @pl.when(jnp.logical_not(is_owner))
+    def _():
+        bytes_of(part, part_ss).wait()
 
     @pl.when(rw_at != s)
     def _():
         rw_copy().wait_send()
 
-    for entry in infos:
-        info_copy(*entry).wait_send()
-
-    for entry in infos:
-        info_arrived(*entry).wait_recv()
+    for i, dst in enumerate((len_recv, hor_recv)):
+        bytes_of(dst.at[pl.ds(0, nb - 1)], info_ss.at[i]).wait()
+        bytes_of(dst.at[pl.ds(0, nb - 1)], info_rs.at[i]).wait()
     lane = lax.broadcasted_iota(jnp.int32, (R, LANES), 1)
     group_out = half * gb + (b * width) // LANES
     local = group_out * LANES + lane
@@ -324,21 +320,23 @@
 
     @pl.when(is_owner)
     def _():
-        each_sum(lambda copy: copy.wait_send())
-        for h in range(per):
-            for j in range(1, nb):
-                tok_copy(h, j).wait_send()
-
-            @pl.when(mine * per + h != s)
-            def _():
-                tok_copy(h, 0).wait_send()
-
-    for o in range(owners):
-        for c in range(nb):
-            pltpu.make_async_remote_copy(
-                sum_send, sum_recv.at[o, c], sum_ss.at[0, 0], sum_rs.at[o, c],
-                device_id={"seq": base + o, "batch": c},
-                device_id_type=pl.DeviceIdType.MESH).wait_recv()
+        bytes_of(sum_all.at[pl.ds(0, n * nb - 1)], sum_ss).wait()
+
+        @pl.when(s // per == mine)
+        def _():
+            bytes_of(tok_all.at[pl.ds(0, per * nb - 1)], tok_ss).wait()
+
+        @pl.when(s // per != mine)
+        def _():
+            bytes_of(tok_all, tok_ss).wait()
+
+    @pl.when(is_owner)
+    def _():
+        bytes_of(sum_all.at[pl.ds(0, owners * nb - 1)], sum_rs).wait()
+
+    @pl.when(jnp.logical_not(is_owner))
+    def _():
+        bytes_of(sum_recv, sum_rs).wait()
 
     acc = jnp.zeros((R, LANES), F32)
     entering = []
@@ -364,11 +362,13 @@
     var = jnp.maximum(second / count - mean * mean, 1.0)
     scale = lax.rsqrt(var)
 
-    for c in range(nb):
-        pltpu.make_async_remote_copy(
-            tok_send.at[0], tok_recv.at[c], tok_ss.at[0, 0], tok_rs.at[c],
-            device_id={"seq": rw_at, "batch": c},
-            device_id_type=pl.DeviceIdType.MESH).wait_recv()
+    @pl.when(rw_at == s)
+    def _():
+        bytes_of(tok_recv.at[pl.ds(0, nb - 1)], tok_rs).wait()
+
+    @pl.when(rw_at != s)
+    def _():
+        bytes_of(tok_recv, tok_rs).wait()
     spots = LANES // width
     spot = b % spots
 
@@ -421,11 +421,13 @@
             pltpu.VMEM((G, 2, R, LANES), F32),
             pltpu.VMEM((nb, 2, R, LANES), F32),
             dma((owners, R)), dma((6,)),
-            dma((owners,)), dma((n,)),
-            dma(()), dma((per,)),
-            dma((2, nb)), dma((2, nb)),
-            dma((n, nb)), dma((owners, nb)),
-            dma((per, nb)), dma((nb,)),
+            dma(()), dma(()),
+            dma(()), dma(()),
+            dma((2,)), dma((2,)),
+            dma(()), dma(()),
+            dma(()), dma(()),
+            pltpu.VMEM((n * nb, R, LANES), F32),
+            pltpu.VMEM((per * nb, 2, R, LANES), F32),
         ],
         compiler_params=pltpu.CompilerParams(collective_id=0, has_side_effects=True),
     )(hidden, gain, weight, rewards, mask, lengths, horizon)

time: 17.5 us -> 16.7 us (0.954)
  Pallas kernels: 16.1 us -> 15.3 us
    pallas_call x1, Pallas kernels: 16.1 us -> 15.3 us  [per_device(): pl.pallas_call(functools.partial(kernel, n, nb, owners), out_shape=pltpu....]
where the time goes in v1:
time: 16.7 us; the launch traced here: 16.6 us
  Pallas kernels  15.3 us (92%)
  between operations  0.64 us (4%)
  local copies, waits for them, and re-layouts  0.6 us (4%)
    pallas_call x1, Pallas kernels, per_device(): pl.pallas_call(functools.partial(kernel, n, nb, owners), out_shape=pltpu....  15.3 us
    slice x1, local copies, waits for them, and re-layouts, per_device(): return (both[:R * nb], both[R * nb:])  0.6 us

profile of v1, /device:TPU:0, one launch (start us, length us, event | category | flops | bytes accessed | tf_op | source)
XLA Modules:
  0.0 16.6 jit_solution(16997276370000652967)
XLA Ops:
  0.6 15.3 %shard_map.86 = f32[16,64]{1,0:T(8,128)S(1)} custom-call(bf16[2,2048,512]{2,1,0:T(8,128)(2,1)} %hidden.1, f32[512]{0:T(512)} %gain.1, f32[512]{0:T(512)} %weight.1, f32[2,256]{1,0:T(2,128)} %rewards.1, s32[2,256]{1,0:T(2,128)} %mask.1, s32[2]{0:T(128)} %lengths.1, f32[2]{0:T(128)} %horizon.1), custom_call_target="tpu_custom_call" | custom-call | tf_op jit(solution)/shard_map/pallas_call | solution.py:398
  16.0 0.6 %fusion = (f32[8,64]{1,0:T(8,128)}, f32[8,64]{1,0:T(8,128)}) fusion(f32[16,64]{1,0:T(8,128)S(1)} %shard_map.86), kind=kLoop, calls=%fused_computation | loop fusion | bytes 8192 | tf_op jit(solution)/shard_map/slice | solution.py:434

commit v2 on v1

v2 whole, which is shorter than its diff:
```python
import functools

import jax
import jax.numpy as jnp
from jax import lax
from jax.experimental import pallas as pl
from jax.experimental.pallas import tpu as pltpu
from jax.sharding import PartitionSpec as P

EPS = 1e-05
LANES = 128
F32 = jnp.float32
MESH = pl.DeviceIdType.MESH


def bytes_of(ref, sem):
    return pltpu.make_async_copy(ref, ref, sem)


def stack(pieces):
    return pieces[0] if len(pieces) == 1 else jnp.concatenate(pieces, 0)


def kernel(n, nb, pair, owners, hidden, gain, weight, rewards, mask, lengths, horizon,
           out_ref,
           hv, gain_v, weight_v, rew_v, mask_v, len_s, hor_s,
           part, rbuf, rw_send, rw_recv, len_send, len_recv, hor_send, hor_recv,
           sum_send, sum_recv, tok_send, tok_recv, sum_all, tok_all,
           chunk_sem, small_sem, part_ss, part_rs, rw_ss, rw_rs, info_ss, info_rs,
           sum_ss, sum_rs, tok_ss, tok_rs):
    R, T, depth = hidden.shape
    block = rewards.shape[1]
    width = block // nb
    per = n // owners
    base = (n - owners) // 2
    L = T // owners
    G = L // LANES
    gb = block // LANES
    rows = G * R
    Q = pair * R
    pairs = nb // pair
    total = depth * n
    s = lax.axis_index("seq")
    b = lax.axis_index("batch")
    side = b % pair
    mate = b // pair
    lead = mate * pair + pair - 1
    is_owner = (s >= base) & (s < base + owners) & (side == pair - 1)
    mine = s - base
    out_o = s // per
    half = s % per
    rw_at = base + out_o

    def chunk_copy(o):
        span = pl.ds(o * L, L)
        return pltpu.make_async_copy(hidden.at[:, span, :], hv.at[:, span, :], chunk_sem.at[o])

    smalls = [
        pltpu.make_async_copy(src, dst, small_sem.at[i])
        for i, (src, dst) in enumerate(
            ((gain, gain_v), (weight, weight_v), (rewards, rew_v), (mask, mask_v),
             (lengths, len_s), (horizon, hor_s)))
    ]
    for copy in smalls:
        copy.start()
    near_high = s * (owners // 2) // n
    near_low = s % 2

    def turn(k):
        back = owners - 1 - k
        if owners % 2:
            return (s + back) % owners
        return (near_high + back // 2) % (owners // 2) * 2 + (near_low + back) % 2

    for k in range(owners):
        chunk_copy(turn(k)).start()
    barrier = pltpu.get_barrier_semaphore()
    for k in range(1, nb):
        pl.semaphore_signal(barrier, inc=1, device_id={"batch": lax.rem(b + k, nb)},
                            device_id_type=MESH)

    @pl.when(is_owner)
    def _():
        for k in range(n):
            for c in range(pair):
                if k or c:
                    pl.semaphore_signal(
                        barrier, inc=1,
                        device_id={"seq": (s + k) % n, "batch": mate * pair + (side + c) % pair},
                        device_id_type=MESH)

    smalls[0].wait()
    smalls[1].wait()
    head = (gain_v[...] * weight_v[...]).reshape(1, depth)
    high = head.astype(jnp.bfloat16).astype(F32)
    middle = (head - high).astype(jnp.bfloat16).astype(F32)
    low = head - high - middle
    wrow = lax.broadcasted_iota(jnp.int32, (16, depth), 0)
    pieces = jnp.where(wrow == 0, high, jnp.where(wrow == 1, middle, jnp.where(wrow == 2, low, 0.0)))
    pieces = pieces.astype(jnp.bfloat16)

    def part_copy(o):
        return pltpu.make_async_remote_copy(
            part.at[o], rbuf.at[s * pair + side], part_ss, part_rs,
            device_id={"seq": base + o, "batch": lead}, device_id_type=MESH)

    def rw_copy():
        return pltpu.make_async_remote_copy(
            rw_send, rw_recv.at[side * per + half], rw_ss, rw_rs,
            device_id={"seq": rw_at, "batch": lead}, device_id_type=MESH)

    def info_copy(k, i, src, dst):
        return pltpu.make_async_remote_copy(
            src, dst.at[b], info_ss.at[i], info_rs.at[i],
            device_id={"batch": lax.rem(b + k, nb)}, device_id_type=MESH)

    infos = ((len_send, len_recv), (hor_send, hor_recv))
    own_rw = is_owner & (mine == out_o)

    def send_part(o):
        @pl.when(jnp.logical_not(is_owner & (mine == o)))
        def _():
            part_copy(o).start()

    meet = min(1, owners - 1)

    def compute(k, carry):
        o = turn(k)
        chunk_copy(o).wait()
        for g in range(G):
            for r in range(R):
                at = pl.ds(pl.multiple_of(o * L + g * LANES, LANES), LANES)
                h = hv[r, at, :]
                sums = lax.dot_general(pieces, h, (((1,), (1,)), ((), ())),
                                       preferred_element_type=F32)
                squares = jnp.zeros((LANES, LANES), F32)
                for j in range(depth // LANES):
                    wide = h[:, j * LANES:(j + 1) * LANES].astype(F32)
                    squares = squares + wide * wide
                row = g * R + r
                part[o, 0, row:row + 1, :] = jnp.sum(sums[0:8], 0, keepdims=True)
                part[o, 1, row:row + 1, :] = jnp.sum(squares.T, 0, keepdims=True)

        @pl.when(k == meet)
        def _():
            for copy in smalls[2:]:
                copy.wait()
            rw = rew_v[...] * mask_v[...].astype(F32)
            for g in range(gb):
                rw_send[g * R:(g + 1) * R, :] = rw[:, g * LANES:(g + 1) * LANES]
            for r in range(R):
                len_send[r:r + 1, :] = jnp.full((1, LANES), len_s[r], jnp.int32)
                hor_send[r:r + 1, :] = jnp.full((1, LANES), hor_s[r], F32)
            met = jnp.where(is_owner, owners - 1, owners) + nb - 1
            pl.semaphore_wait(barrier, met)
            for before in range(meet):
                send_part(turn(before))

            @pl.when(jnp.logical_not(own_rw))
            def _():
                rw_copy().start()

            for j in range(1, nb):
                for i, (src, dst) in enumerate(infos):
                    info_copy(j, i, src, dst).start()

        @pl.when(k >= meet)
        def _():
            send_part(o)
        return carry

    lax.fori_loop(0, owners, compute, 0)

    @pl.when(own_rw)
    def _():
        rw_recv[side * per + half] = rw_send[...]

    len_recv[b] = len_send[...]
    hor_recv[b] = hor_send[...]
    for i, (src, dst) in enumerate(infos):
        bytes_of(dst.at[pl.ds(0, nb - 1)], info_rs.at[i]).wait()

    def sum_copy(i, j):
        return pltpu.make_async_remote_copy(
            sum_send, sum_recv.at[mine * pairs + mate], sum_ss, sum_rs,
            device_id={"seq": i, "batch": j}, device_id_type=MESH)

    def each_sum():
        def one(i):
            for j in range(nb):
                never = isinstance(i, int) and not base <= i < base + owners
                if never or j % pair != pair - 1:
                    sum_copy(i, j).start()
                else:
                    @pl.when((i != s) | (j != b))
                    def _():
                        sum_copy(i, j).start()

        if n * nb <= 32:
            for i in range(n):
                one(i)
        else:
            def body(i, carry):
                one(i)
                return carry
            lax.fori_loop(0, n, body, 0)

    def tok_copy(h, j):
        return pltpu.make_async_remote_copy(
            tok_send.at[h * gb + (j * width) // LANES], tok_recv.at[mate], tok_ss, tok_rs,
            device_id={"seq": mine * per + h, "batch": j}, device_id_type=MESH)

    @pl.when(is_owner)
    def _():
        row = lax.broadcasted_iota(jnp.int32, (pair * rows, LANES), 0)
        lane = lax.broadcasted_iota(jnp.int32, (pair * rows, LANES), 1)
        group = row % rows // R
        length = stack([len_recv[mate * pair + c] for c in range(pair) for _ in range(G)])
        reach = stack([hor_recv[mate * pair + c] for c in range(pair) for _ in range(G)])
        rate = -1.0 / reach
        local = group * LANES + lane
        valid = (mine * L + local < length).astype(F32)
        step = 16
        near = [jnp.where(lane < LANES - k, jnp.exp(rate * (k - 1)), 0.0) for k in range(1, step + 1)]
        far = [jnp.where(lane < LANES - k, jnp.exp(rate * k), 0.0) for k in range(step, LANES, step)]
        lead_in = jnp.exp(rate * lane.astype(F32))
        hops = [1 << i for i in range(max(G - 1, 0).bit_length())]
        row_decay = [jnp.where(group + k < G, jnp.exp(rate * (k * LANES)), 0.0) for k in hops]
        into = jnp.where(group < G - 1, jnp.exp(rate * (LANES - 1 - lane).astype(F32)), 0.0)
        power = jnp.exp(rate * (L - 1 - local).astype(F32))
        decay = jnp.exp(rate)
        power_sum = jnp.sum(power, 1, keepdims=True)
        power_squares = jnp.sum(power * power, 1, keepdims=True)
        fixed = jnp.where(lane == 4, power_sum, jnp.where(lane == 5, power_squares, 0.0))

        @pl.when(own_rw)
        def _():
            if pair * per > 1:
                bytes_of(rw_recv.at[pl.ds(0, pair * per - 1)], rw_rs).wait()

        @pl.when(jnp.logical_not(own_rw))
        def _():
            bytes_of(rw_recv, rw_rs).wait()
        gains = stack([rw_recv[c * per + h] for c in range(pair) for h in range(per)])

        rbuf[s * pair + side] = part[mine]
        bytes_of(rbuf.at[pl.ds(0, n * pair - 1)], part_rs).wait()
        projected, squares = [], []
        for c in range(pair):
            first, second = rbuf[c, 0], rbuf[c, 1]
            for k in range(1, n):
                first = first + rbuf[k * pair + c, 0]
                second = second + rbuf[k * pair + c, 1]
            projected.append(first)
            squares.append(second)
        values = stack(projected) * lax.rsqrt(stack(squares) / total + EPS)
        held = values * valid
        change = (gains - values) * valid
        mixed = decay * change + held
        start = jnp.sum(lead_in * mixed, 1, keepdims=True)
        terms = [factor * pltpu.roll(mixed if k < step else held, LANES - k, 1)
                 for k, factor in enumerate(near, 1)]
        while len(terms) > 1:
            terms = [sum(terms[i + 1:i + 2], terms[i]) for i in range(0, len(terms), 2)]
        gae = change + terms[0]
        terms = [factor * pltpu.roll(gae, LANES - k * step, 1) for k, factor in enumerate(far, 1)]
        while len(terms) > 1:
            terms = [sum(terms[i + 1:i + 2], terms[i]) for i in range(0, len(terms), 2)]
        gae = gae + terms[0]
        start = jnp.broadcast_to(start, gae.shape)
        if G > 1:
            for k, factor in zip(hops, row_decay):
                start = start + factor * pltpu.roll(start, pair * rows - k * R, 0)
            gae = gae + into * pltpu.roll(start, pair * rows - R, 0)
        sums = jnp.where(lane == 1, jnp.sum(gae, 1, keepdims=True), fixed)
        sums = jnp.where(lane == 2, 2.0 * jnp.sum(gae * power, 1, keepdims=True), sums)
        sums = jnp.where(lane == 3, jnp.sum(gae * gae, 1, keepdims=True), sums)
        sums = jnp.where((lane == 0) & (group == 0), start, sums)
        for c in range(pair):
            summary = sums[c * rows:c * rows + R]
            for g in range(1, G):
                summary = summary + sums[c * rows + g * R:c * rows + (g + 1) * R]
            sum_send[c * R:(c + 1) * R, :] = summary
        sum_recv[mine * pairs + mate] = sum_send[...]
        each_sum()
        for g in range(G):
            for c in range(pair):
                at = c * rows + g * R
                tok_send[g, 0, c * R:(c + 1) * R, :] = gae[at:at + R]
                tok_send[g, 1, c * R:(c + 1) * R, :] = values[at:at + R]
        for h in range(per):
            for j in range(nb):
                if j % pair != pair - 1:
                    tok_copy(h, j).start()
                else:
                    @pl.when((mine * per + h != s) | (j != b))
                    def _():
                        tok_copy(h, j).start()

                    @pl.when((mine * per + h == s) & (j == b))
                    def _():
                        tok_recv[mate] = tok_send[h * gb + (j * width) // LANES]

    @pl.when(is_owner)
    def _():
        if owners > 1:
            bytes_of(part.at[pl.ds(0, owners - 1)], part_ss).wait()

    @pl.when(jnp.logical_not(is_owner))
    def _():
        bytes_of(part, part_ss).wait()

    @pl.when(jnp.logical_not(own_rw))
    def _():
        rw_copy().wait_send()

    for i, (src, dst) in enumerate(infos):
        bytes_of(dst.at[pl.ds(0, nb - 1)], info_ss.at[i]).wait()

    spots = LANES // width
    spot = b % spots

    def pick(x):
        result = x[:, 0:width]
        for j in range(1, spots):
            result = jnp.where(spot == j, x[:, j * width:(j + 1) * width], result)
        return result

    every = nb * R
    lane = lax.broadcasted_iota(jnp.int32, (every, LANES), 1)
    local = (half * gb + (b * width) // LANES) * LANES + lane
    length = stack([len_recv[c] for c in range(nb)])
    rate = -1.0 / stack([hor_recv[c] for c in range(nb)])
    count = jnp.sum(jnp.minimum(length, T).astype(F32), 0, keepdims=True)
    jump = jnp.exp(rate * float(L))
    power_out = pick(jnp.exp(rate * (L - 1 - local).astype(F32)))
    valid_out = pick((out_o * L + local < length).astype(F32))

    @pl.when(is_owner)
    def _():
        bytes_of(sum_all.at[pl.ds(0, n * nb - 1)], sum_ss).wait()

    @pl.when(own_rw)
    def _():
        bytes_of(tok_all.at[pl.ds(0, per * nb - 1)], tok_ss).wait()

    @pl.when(is_owner & jnp.logical_not(own_rw))
    def _():
        bytes_of(tok_all, tok_ss).wait()

    @pl.when(is_owner)
    def _():
        bytes_of(sum_all.at[pl.ds(0, owners * pairs - 1)], sum_rs).wait()

    @pl.when(jnp.logical_not(is_owner))
    def _():
        bytes_of(sum_recv, sum_rs).wait()

    @pl.when(own_rw)
    def _():
        if pairs > 1:
            bytes_of(tok_recv.at[pl.ds(0, pairs - 1)], tok_rs).wait()

    @pl.when(jnp.logical_not(own_rw))
    def _():
        bytes_of(tok_recv, tok_rs).wait()

    gae = pick(stack([tok_recv[c, 0] for c in range(pairs)]))
    values = pick(stack([tok_recv[c, 1] for c in range(pairs)]))
    acc = jnp.zeros((every, LANES), F32)
    u = jnp.zeros((every, LANES), F32)
    entering = jnp.zeros((every, LANES), F32)
    for o in reversed(range(owners)):
        message = stack([sum_recv[o * pairs + c] for c in range(pairs)])
        factor = jnp.where((lane == 1) | (lane == 3), 1.0,
                           jnp.where((lane == 2) | (lane == 4), u,
                                     jnp.where(lane == 5, u * u, 0.0)))
        acc = acc + message * factor
        entering = jnp.where(out_o == o, u, entering)
        if o:
            u = jnp.broadcast_to(message[:, 0:1], (every, LANES)) + jump * u
    acc = jnp.sum(acc, 0, keepdims=True)
    lane1 = lax.broadcasted_iota(jnp.int32, (1, LANES), 1)
    first = jnp.sum(jnp.where((lane1 == 1) | (lane1 == 4), acc, 0.0), 1, keepdims=True)
    second = jnp.sum(jnp.where((lane1 == 2) | (lane1 == 3) | (lane1 == 5), acc, 0.0), 1, keepdims=True)
    mean = first / count[:, 0:1]
    var = jnp.maximum(second / count[:, 0:1] - mean * mean, 1.0)
    scale = lax.rsqrt(var)
    gae = gae + power_out * entering[:, 0:width]
    out_ref[every:2 * every, :] = (gae + values) * valid_out
    out_ref[0:every, :] = (gae - mean) * valid_out * scale


def per_device(hidden, gain, weight, rewards, mask, lengths, horizon):
    n = lax.axis_size("seq")
    nb = lax.axis_size("batch")
    pair = 2 - nb % 2
    owners = n // 2 if n % 4 == 0 else n
    R, T, depth = hidden.shape
    block = rewards.shape[1]
    per = n // owners
    G = T // owners // LANES
    gb = block // LANES
    rows = G * R
    Q = pair * R
    pairs = nb // pair
    dma = pltpu.SemaphoreType.DMA
    both = pl.pallas_call(
        functools.partial(kernel, n, nb, pair, owners),
        out_shape=pltpu.VMEM((2 * R * nb, block // nb), F32),
        in_specs=[pl.BlockSpec(memory_space=pl.ANY)] * 7,
        out_specs=pl.BlockSpec(memory_space=pltpu.VMEM),
        scratch_shapes=[
            pltpu.VMEM((R, T, depth), jnp.bfloat16),
            pltpu.VMEM((depth,), F32),
            pltpu.VMEM((depth,), F32),
            pltpu.VMEM((R, block), F32),
            pltpu.VMEM((R, block), jnp.int32),
            pltpu.SMEM((R,), jnp.int32),
            pltpu.SMEM((R,), F32),
            pltpu.VMEM((owners, 2, rows, LANES), F32),
            pltpu.VMEM((n * pair, 2, rows, LANES), F32),
            pltpu.VMEM((gb * R, LANES), F32),
            pltpu.VMEM((pair * per, gb * R, LANES), F32),
            pltpu.VMEM((R, LANES), jnp.int32),
            pltpu.VMEM((nb, R, LANES), jnp.int32),
            pltpu.VMEM((R, LANES), F32),
            pltpu.VMEM((nb, R, LANES), F32),
            pltpu.VMEM((Q, LANES), F32),
            pltpu.VMEM((owners * pairs, Q, LANES), F32),
            pltpu.VMEM((G, 2, Q, LANES), F32),
            pltpu.VMEM((pairs, 2, Q, LANES), F32),
            pltpu.VMEM((n * nb, Q, LANES), F32),
            pltpu.VMEM((per * nb, 2, Q, LANES), F32),
            dma((owners,)), dma((6,)),
            dma(()), dma(()),
            dma(()), dma(()),
            dma((2,)), dma((2,)),
            dma(()), dma(()),
            dma(()), dma(()),
        ],
        compiler_params=pltpu.CompilerParams(collective_id=0, has_side_effects=True),
    )(hidden, gain, weight, rewards, mask, lengths, horizon)
    return both[:R * nb], both[R * nb:]


def solution(mesh):
    return jax.shard_map(
        per_device,
        mesh=mesh,
        in_specs=(
            P("batch", None, "seq"),
            P("seq"),
            P("seq"),
            P("batch", "seq"),
            P("batch", "seq"),
            P("batch"),
            P("batch"),
        ),
        out_specs=(P(None, ("seq", "batch")), P(None, ("seq", "batch"))),
        check_vma=False,
    )
```

time: 16.7 us -> 15.1 us (0.904)
  Pallas kernels: 15.3 us -> 13.7 us
    pallas_call x1, Pallas kernels: 15.3 us -> 13.7 us  [per_device(): pl.pallas_call(functools.partial(kernel, n, nb, pair, owners), out_shape=...]
where the time goes in v2:
time: 15.1 us; the launch traced here: 14.9 us
  Pallas kernels  13.7 us (91%)
  between operations  0.64 us (4%)
  local copies, waits for them, and re-layouts  0.6 us (4%)
    pallas_call x1, Pallas kernels, per_device(): pl.pallas_call(functools.partial(kernel, n, nb, pair, owners), out_shape=...  13.7 us
    slice x1, local copies, waits for them, and re-layouts, per_device(): return (both[:R * nb], both[R * nb:])  0.6 us

profile of v2, /device:TPU:0, one launch (start us, length us, event | category | flops | bytes accessed | tf_op | source)
XLA Modules:
  0.0 14.9 jit_solution(14493664875887056107)
XLA Ops:
  0.6 13.7 %shard_map.86 = f32[16,64]{1,0:T(8,128)S(1)} custom-call(bf16[2,2048,512]{2,1,0:T(8,128)(2,1)} %hidden.1, f32[512]{0:T(512)} %gain.1, f32[512]{0:T(512)} %weight.1, f32[2,256]{1,0:T(2,128)} %rewards.1, s32[2,256]{1,0:T(2,128)} %mask.1, s32[2]{0:T(128)} %lengths.1, f32[2]{0:T(128)} %horizon.1), custom_call_target="tpu_custom_call" | custom-call | tf_op jit(solution)/shard_map/pallas_call | solution.py:408
  14.3 0.6 %fusion = (f32[8,64]{1,0:T(8,128)}, f32[8,64]{1,0:T(8,128)}) fusion(f32[16,64]{1,0:T(8,128)S(1)} %shard_map.86), kind=kLoop, calls=%fused_computation | loop fusion | bytes 8192 | tf_op jit(solution)/shard_map/slice | solution.py:444

commit v3 on v2

--- a/solution.py
+++ b/solution.py
@@ -9,6 +9,7 @@
 
 EPS = 1e-05
 LANES = 128
+TILE = 256
 F32 = jnp.float32
 MESH = pl.DeviceIdType.MESH
 
@@ -21,11 +22,11 @@
     return pieces[0] if len(pieces) == 1 else jnp.concatenate(pieces, 0)
 
 
-def kernel(n, nb, pair, owners, hidden, gain, weight, rewards, mask, lengths, horizon,
+def kernel(n, nb, pair, owners, subs, hidden, gain, weight, rewards, mask, lengths, horizon,
            out_ref,
            hv, gain_v, weight_v, rew_v, mask_v, len_s, hor_s,
            part, rbuf, rw_send, rw_recv, len_send, len_recv, hor_send, hor_recv,
-           sum_send, sum_recv, tok_send, tok_recv, sum_all, tok_all,
+           sum_send, sum_recv, tok_send, tok_recv, sum_all, tok_all, held_squares,
            chunk_sem, small_sem, part_ss, part_rs, rw_ss, rw_rs, info_ss, info_rs,
            sum_ss, sum_rs, tok_ss, tok_rs):
     R, T, depth = hidden.shape
@@ -51,9 +52,11 @@
     half = s % per
     rw_at = base + out_o
 
-    def chunk_copy(o):
-        span = pl.ds(o * L, L)
-        return pltpu.make_async_copy(hidden.at[:, span, :], hv.at[:, span, :], chunk_sem.at[o])
+    S = L // subs
+
+    def chunk_copy(o, j):
+        span = pl.ds(o * L + j * S, S)
+        return pltpu.make_async_copy(hidden.at[:, span, :], hv.at[:, span, :], chunk_sem.at[o, j])
 
     smalls = [
         pltpu.make_async_copy(src, dst, small_sem.at[i])
@@ -73,7 +76,8 @@
         return (near_high + back // 2) % (owners // 2) * 2 + (near_low + back) % 2
 
     for k in range(owners):
-        chunk_copy(turn(k)).start()
+        for j in range(subs):
+            chunk_copy(turn(k), j).start()
     barrier = pltpu.get_barrier_semaphore()
     for k in range(1, nb):
         pl.semaphore_signal(barrier, inc=1, device_id={"batch": lax.rem(b + k, nb)},
@@ -124,52 +128,111 @@
 
     meet = min(1, owners - 1)
 
+    def enter():
+        for copy in smalls[2:]:
+            copy.wait()
+        rw = rew_v[...] * mask_v[...].astype(F32)
+        for g in range(gb):
+            rw_send[g * R:(g + 1) * R, :] = rw[:, g * LANES:(g + 1) * LANES]
+        for r in range(R):
+            len_send[r:r + 1, :] = jnp.full((1, LANES), len_s[r], jnp.int32)
+            hor_send[r:r + 1, :] = jnp.full((1, LANES), hor_s[r], F32)
+        met = jnp.where(is_owner, owners - 1, owners) + nb - 1
+        pl.semaphore_wait(barrier, met)
+        for before in range(meet):
+            send_part(turn(before))
+
+        @pl.when(jnp.logical_not(own_rw))
+        def _():
+            rw_copy().start()
+
+        for j in range(1, nb):
+            for i, (src, dst) in enumerate(infos):
+                info_copy(j, i, src, dst).start()
+
+    def squares_of(h):
+        squares = jnp.zeros((h.shape[0], LANES), F32)
+        for j in range(depth // LANES):
+            wide = h[:, j * LANES:(j + 1) * LANES].astype(F32)
+            squares = squares + wide * wide
+        return squares
+
     def compute(k, carry):
         o = turn(k)
-        chunk_copy(o).wait()
+        for j in range(subs):
+            chunk_copy(o, j).wait()
         for g in range(G):
             for r in range(R):
                 at = pl.ds(pl.multiple_of(o * L + g * LANES, LANES), LANES)
                 h = hv[r, at, :]
                 sums = lax.dot_general(pieces, h, (((1,), (1,)), ((), ())),
                                        preferred_element_type=F32)
-                squares = jnp.zeros((LANES, LANES), F32)
-                for j in range(depth // LANES):
-                    wide = h[:, j * LANES:(j + 1) * LANES].astype(F32)
-                    squares = squares + wide * wide
                 row = g * R + r
                 part[o, 0, row:row + 1, :] = jnp.sum(sums[0:8], 0, keepdims=True)
-                part[o, 1, row:row + 1, :] = jnp.sum(squares.T, 0, keepdims=True)
+                part[o, 1, row:row + 1, :] = jnp.sum(squares_of(h).T, 0, keepdims=True)
 
         @pl.when(k == meet)
         def _():
-            for copy in smalls[2:]:
-                copy.wait()
-            rw = rew_v[...] * mask_v[...].astype(F32)
-            for g in range(gb):
-                rw_send[g * R:(g + 1) * R, :] = rw[:, g * LANES:(g + 1) * LANES]
-            for r in range(R):
-                len_send[r:r + 1, :] = jnp.full((1, LANES), len_s[r], jnp.int32)
-                hor_send[r:r + 1, :] = jnp.full((1, LANES), hor_s[r], F32)
-            met = jnp.where(is_owner, owners - 1, owners) + nb - 1
-            pl.semaphore_wait(barrier, met)
-            for before in range(meet):
-                send_part(turn(before))
-
-            @pl.when(jnp.logical_not(own_rw))
-            def _():
-                rw_copy().start()
-
-            for j in range(1, nb):
-                for i, (src, dst) in enumerate(infos):
-                    info_copy(j, i, src, dst).start()
+            enter()
 
         @pl.when(k >= meet)
         def _():
             send_part(o)
         return carry
 
-    lax.fori_loop(0, owners, compute, 0)
+    tiles = depth // TILE
+
+    def unit(r, m):
+        return (r * tiles + m) % 2
+
+    def streamed(*accs):
+        def acc_of(step, r, m):
+            return accs[(step % 2 * R + r) * 2 + unit(r, m)]
+
+        def used(step, r):
+            return [accs[(step % 2 * R + r) * 2 + q]
+                    for q in sorted({unit(r, m) for m in range(tiles)})]
+
+        for step in range(2):
+            for r in range(R):
+                for acc in used(step, r):
+                    pltpu.matmul_pop(acc)
+        for step in range(owners * subs + 1):
+            if step < owners * subs:
+                o, j = turn(step // subs), step % subs
+                chunk_copy(o, j).wait()
+                for r in range(R):
+                    h = hv[r, pl.ds(pl.multiple_of(o * L + j * S, S), S), :]
+                    for m in range(tiles):
+                        cols = slice(m * TILE, (m + 1) * TILE)
+                        pltpu.matmul_push_rhs(h[:, cols], staging_register=r % 2,
+                                              mxu_index=unit(r, m), transpose=True)
+                        pltpu.matmul_acc_lhs(acc_of(step, r, m), pieces[:, cols],
+                                             load_staged_rhs=r % 2)
+                    held_squares[step % 2, r] = squares_of(h)
+            if step:
+                last = step - 1
+                o, j = turn(last // subs), last % subs
+                for r in range(R):
+                    sums = 0.0
+                    for acc in used(last, r):
+                        sums = sums + pltpu.matmul_pop(acc)
+                    sums = jnp.sum(sums[0:8], 0, keepdims=True)
+                    for g in range(S // LANES):
+                        row = (j * (S // LANES) + g) * R + r
+                        square = held_squares[last % 2, r, g * LANES:(g + 1) * LANES, :]
+                        part[o, 0, row:row + 1, :] = sums[:, g * LANES:(g + 1) * LANES]
+                        part[o, 1, row:row + 1, :] = jnp.sum(square.T, 0, keepdims=True)
+                if j == subs - 1:
+                    if last // subs == meet:
+                        enter()
+                    if last // subs >= meet:
+                        send_part(o)
+
+    if depth % TILE == 0 and S == TILE:
+        pl.run_scoped(streamed, *[pltpu.ACC(i % 2)((16, TILE), F32) for i in range(4 * R)])
+    else:
+        lax.fori_loop(0, owners, compute, 0)
 
     @pl.when(own_rw)
     def _():
@@ -397,6 +460,7 @@
     pair = 2 - nb % 2
     owners = n // 2 if n % 4 == 0 else n
     R, T, depth = hidden.shape
+    subs = max(T // owners // TILE, 1)
     block = rewards.shape[1]
     per = n // owners
     G = T // owners // LANES
@@ -406,7 +470,7 @@
     pairs = nb // pair
     dma = pltpu.SemaphoreType.DMA
     both = pl.pallas_call(
-        functools.partial(kernel, n, nb, pair, owners),
+        functools.partial(kernel, n, nb, pair, owners, subs),
         out_shape=pltpu.VMEM((2 * R * nb, block // nb), F32),
         in_specs=[pl.BlockSpec(memory_space=pl.ANY)] * 7,
         out_specs=pl.BlockSpec(memory_space=pltpu.VMEM),
@@ -432,7 +496,8 @@
             pltpu.VMEM((pairs, 2, Q, LANES), F32),
             pltpu.VMEM((n * nb, Q, LANES), F32),
             pltpu.VMEM((per * nb, 2, Q, LANES), F32),
-            dma((owners,)), dma((6,)),
+            pltpu.VMEM((2, R, TILE, LANES), F32),
+            dma((owners, subs)), dma((6,)),
             dma(()), dma(()),
             dma(()), dma(()),
             dma((2,)), dma((2,)),

time: 15.1 us -> 14.7 us (0.974)
  Pallas kernels: 13.7 us -> 13.3 us
    pallas_call x1, Pallas kernels: 13.7 us -> 13.3 us  [per_device(): pl.pallas_call(functools.partial(kernel, n, nb, pair, owners, subs), out_...]
where the time goes in v3:
time: 14.7 us; the launch traced here: 14.5 us
  Pallas kernels  13.3 us (90%)
  between operations  0.64 us (4%)
  local copies, waits for them, and re-layouts  0.6 us (4%)
    pallas_call x1, Pallas kernels, per_device(): pl.pallas_call(functools.partial(kernel, n, nb, pair, owners, subs), out_...  13.3 us
    slice x1, local copies, waits for them, and re-layouts, per_device(): return (both[:R * nb], both[R * nb:])  0.6 us

profile of v3, /device:TPU:0, one launch (start us, length us, event | category | flops | bytes accessed | tf_op | source)
XLA Modules:
  0.0 14.5 jit_solution(17248966165214508753)
XLA Ops:
  0.6 13.3 %shard_map.86 = f32[16,64]{1,0:T(8,128)S(1)} custom-call(bf16[2,2048,512]{2,1,0:T(8,128)(2,1)} %hidden.1, f32[512]{0:T(512)} %gain.1, f32[512]{0:T(512)} %weight.1, f32[2,256]{1,0:T(2,128)} %rewards.1, s32[2,256]{1,0:T(2,128)} %mask.1, s32[2]{0:T(128)} %lengths.1, f32[2]{0:T(128)} %horizon.1), custom_call_target="tpu_custom_call" | custom-call | tf_op jit(solution)/shard_map/pallas_call | solution.py:472
  13.9 0.6 %fusion = (f32[8,64]{1,0:T(8,128)}, f32[8,64]{1,0:T(8,128)}) fusion(f32[16,64]{1,0:T(8,128)S(1)} %shard_map.86), kind=kLoop, calls=%fused_computation | loop fusion | bytes 8192 | tf_op jit(solution)/shard_map/slice | solution.py:509

commit v4 on v3

v4 whole, which is shorter than its diff:
```python
import functools

import jax
import jax.numpy as jnp
from jax import lax
from jax.experimental import pallas as pl
from jax.experimental.pallas import tpu as pltpu
from jax.sharding import PartitionSpec as P

EPS = 1e-05
LANES = 128
TILE = 256
F32 = jnp.float32
MESH = pl.DeviceIdType.MESH


def bytes_of(ref, sem):
    return pltpu.make_async_copy(ref, ref, sem)


def stack(pieces):
    return pieces[0] if len(pieces) == 1 else jnp.concatenate(pieces, 0)


def kernel(n, nb, pair, owners, subs, stream, hidden, gain, weight, rewards, mask, lengths, horizon,
           out_ref,
           hv, gain_v, weight_v, rew_v, mask_v, len_s, hor_s,
           part, rbuf, rw_send, rw_recv, len_send, len_recv, hor_send, hor_recv,
           sum_send, sum_recv, tok_send, tok_recv, both_v, both_m, any_rows, held_squares,
           chunk_sem, small_sem, sent, early, part_rs, late):
    R, T, depth = hidden.shape
    block = rewards.shape[1]
    width = block // nb
    per = n // owners
    base = (n - owners) // 2
    L = T // owners
    G = L // LANES
    gb = block // LANES
    rows = G * R
    Q = pair * R
    pairs = nb // pair
    total = depth * n
    s = lax.axis_index("seq")
    b = lax.axis_index("batch")
    side = b % pair
    mate = b // pair
    lead = mate * pair + pair - 1
    is_owner = (s >= base) & (s < base + owners) & (side == pair - 1)
    mine = s - base
    out_o = s // per
    half = s % per
    rw_at = base + out_o

    S = L // subs
    srows = rows // subs
    near_high = s * (owners // 2) // n
    near_low = s % 2

    def turn(k):
        back = owners - 1 - k
        if owners % 2:
            return (s + back) % owners
        return (near_high + back // 2) % (owners // 2) * 2 + (near_low + back) % 2

    def chunk_copy(c):
        span = pl.ds(turn(c // subs) * L + c % subs * S, S)
        return pltpu.make_async_copy(hidden.at[:, span, :], hv.at[:, span, :], chunk_sem.at[c])

    def wait_rows(count, sem):
        if count:
            bytes_of(any_rows.at[pl.ds(0, count)], sem).wait()

    pltpu.make_async_copy(gain, gain_v, small_sem.at[0]).start()
    pltpu.make_async_copy(weight, weight_v, small_sem.at[0]).start()
    for c in range(owners * subs):
        chunk_copy(c).start()
    pltpu.make_async_copy(rewards, rew_v, small_sem.at[1]).start()
    pltpu.make_async_copy(mask, mask_v, small_sem.at[1]).start()
    ends = [pltpu.make_async_copy(lengths, len_s, small_sem.at[2]),
            pltpu.make_async_copy(horizon, hor_s, small_sem.at[3])]
    for copy in ends:
        copy.start()
    barrier = pltpu.get_barrier_semaphore()
    for k in range(1, nb):
        pl.semaphore_signal(barrier, inc=1, device_id={"batch": lax.rem(b + k, nb)},
                            device_id_type=MESH)

    @pl.when(is_owner)
    def _():
        for k in range(n):
            for c in range(pair):
                if k or c:
                    pl.semaphore_signal(
                        barrier, inc=1,
                        device_id={"seq": (s + k) % n, "batch": mate * pair + (side + c) % pair},
                        device_id_type=MESH)

    def head_pieces():
        bytes_of(both_v.at[pl.ds(0, 2 * depth)], small_sem.at[0]).wait()
        head = (gain_v[...] * weight_v[...]).reshape(1, depth)
        high = head.astype(jnp.bfloat16).astype(F32)
        middle = (head - high).astype(jnp.bfloat16).astype(F32)
        low = head - high - middle
        wrow = lax.broadcasted_iota(jnp.int32, (16, depth), 0)
        pieces = jnp.where(wrow == 0, high, jnp.where(wrow == 1, middle, jnp.where(wrow == 2, low, 0.0)))
        return pieces.astype(jnp.bfloat16)

    def part_copy(o, j):
        return pltpu.make_async_remote_copy(
            part.at[o, j], rbuf.at[s * pair + side, j], sent, part_rs,
            device_id={"seq": base + o, "batch": lead}, device_id_type=MESH)

    def rw_copy():
        return pltpu.make_async_remote_copy(
            rw_send, rw_recv.at[side * per + half], sent, early,
            device_id={"seq": rw_at, "batch": lead}, device_id_type=MESH)

    def info_copy(k, src, dst):
        return pltpu.make_async_remote_copy(
            src, dst.at[b], sent, early,
            device_id={"batch": lax.rem(b + k, nb)}, device_id_type=MESH)

    infos = ((len_send, len_recv), (hor_send, hor_recv))
    own_rw = is_owner & (mine == out_o)

    def send_part(o, j):
        @pl.when(jnp.logical_not(is_owner & (mine == o)))
        def _():
            part_copy(o, j).start()

    meet = min(2, owners * subs - 1)

    def enter():
        bytes_of(both_m, small_sem.at[1]).wait()
        for copy in ends:
            copy.wait()
        rw = rew_v[...] * mask_v[...].astype(F32)
        for g in range(gb):
            rw_send[g * R:(g + 1) * R, :] = rw[:, g * LANES:(g + 1) * LANES]
        for r in range(R):
            len_send[r:r + 1, :] = jnp.full((1, LANES), len_s[r], jnp.int32)
            hor_send[r:r + 1, :] = jnp.full((1, LANES), hor_s[r], F32)
        met = jnp.where(is_owner, owners - 1, owners) + nb - 1
        pl.semaphore_wait(barrier, met)

        @pl.when(jnp.logical_not(own_rw))
        def _():
            rw_copy().start()

        for j in range(1, nb):
            for src, dst in infos:
                info_copy(j, src, dst).start()

    def squares_of(h):
        squares = jnp.zeros((h.shape[0], LANES), F32)
        for j in range(depth // LANES):
            wide = h[:, j * LANES:(j + 1) * LANES].astype(F32)
            squares = squares + wide * wide
        return squares

    def compute(k, pieces):
        o = turn(k)
        for j in range(subs):
            chunk_copy(k * subs + j).wait()
        for g in range(G):
            for r in range(R):
                at = pl.ds(pl.multiple_of(o * L + g * LANES, LANES), LANES)
                h = hv[r, at, :]
                sums = lax.dot_general(pieces, h, (((1,), (1,)), ((), ())),
                                       preferred_element_type=F32)
                j, row = divmod(g * R + r, srows)
                part[o, j, 0, row:row + 1, :] = jnp.sum(sums[0:8], 0, keepdims=True)
                part[o, j, 1, row:row + 1, :] = jnp.sum(squares_of(h).T, 0, keepdims=True)

        @pl.when(k == 0)
        def _():
            enter()

        for j in range(subs):
            send_part(o, j)
        return pieces

    def streamed(*accs):
        for acc in accs:
            pltpu.matmul_pop(acc)
        pieces = None
        units = [(r, m) for r in range(R) for m in range(2)]
        for step in range(owners * subs + 1):
            if step < owners * subs:
                o, j = turn(step // subs), step % subs
                chunk_copy(step).wait()
                blocks = [hv[r, pl.ds(pl.multiple_of(o * L + j * S, S), S), :] for r in range(R)]
                if step == 0:
                    for r, m in units:
                        pltpu.matmul_push_rhs(blocks[r][:, m * TILE:(m + 1) * TILE],
                                              staging_register=r, mxu_index=m, transpose=True)
                    for r in range(R):
                        held_squares[step % 2, r] = squares_of(blocks[r])
                    pieces = head_pieces()
                for r, m in units:
                    if step:
                        pltpu.matmul_push_rhs(blocks[r][:, m * TILE:(m + 1) * TILE],
                                              staging_register=r, mxu_index=m, transpose=True)
                    pltpu.matmul_acc_lhs(accs[(step % 2 * R + r) * 2 + m],
                                         pieces[:, m * TILE:(m + 1) * TILE], load_staged_rhs=r)
                if step:
                    for r in range(R):
                        held_squares[step % 2, r] = squares_of(blocks[r])
            if step:
                last = step - 1
                o, j = turn(last // subs), last % subs
                for r in range(R):
                    at = (last % 2 * R + r) * 2
                    sums = pltpu.matmul_pop(accs[at]) + pltpu.matmul_pop(accs[at + 1])
                    sums = jnp.sum(sums[0:8], 0, keepdims=True)
                    for g in range(S // LANES):
                        row = g * R + r
                        square = held_squares[last % 2, r, g * LANES:(g + 1) * LANES, :]
                        part[o, j, 0, row:row + 1, :] = sums[:, g * LANES:(g + 1) * LANES]
                        part[o, j, 1, row:row + 1, :] = jnp.sum(square.T, 0, keepdims=True)
                if last == meet:
                    enter()
                for c in range(last if last > meet else 0, last + 1 if last >= meet else 0):
                    send_part(turn(c // subs), c % subs)

    if stream:
        pl.run_scoped(streamed, *[pltpu.ACC(i % 2)((16, TILE), F32) for i in range(4 * R)])
    else:
        lax.fori_loop(0, owners, compute, head_pieces())

    @pl.when(own_rw)
    def _():
        rw_recv[side * per + half] = rw_send[...]

    len_recv[b] = len_send[...]
    hor_recv[b] = hor_send[...]
    info_rows = 2 * R * (nb - 1)

    @pl.when(jnp.logical_not(is_owner))
    def _():
        wait_rows(info_rows, early)

    @pl.when(own_rw)
    def _():
        wait_rows(info_rows + gb * R * (pair * per - 1), early)

    @pl.when(is_owner & jnp.logical_not(own_rw))
    def _():
        wait_rows(info_rows + gb * R * pair * per, early)

    def sum_copy(i, j):
        return pltpu.make_async_remote_copy(
            sum_send, sum_recv.at[mine * pairs + mate], sent, late,
            device_id={"seq": i, "batch": j}, device_id_type=MESH)

    def each_sum():
        def one(i):
            for j in range(nb):
                never = isinstance(i, int) and not base <= i < base + owners
                if never or j % pair != pair - 1:
                    sum_copy(i, j).start()
                else:
                    @pl.when((i != s) | (j != b))
                    def _():
                        sum_copy(i, j).start()

        if n * nb <= 32:
            for i in range(n):
                one(i)
        else:
            def body(i, carry):
                one(i)
                return carry
            lax.fori_loop(0, n, body, 0)

    def tok_copy(h, j):
        return pltpu.make_async_remote_copy(
            tok_send.at[h * gb + (j * width) // LANES], tok_recv.at[mate], sent, late,
            device_id={"seq": mine * per + h, "batch": j}, device_id_type=MESH)

    @pl.when(is_owner)
    def _():
        row = lax.broadcasted_iota(jnp.int32, (pair * rows, LANES), 0)
        lane = lax.broadcasted_iota(jnp.int32, (pair * rows, LANES), 1)
        group = row % rows // R
        length = stack([len_recv[mate * pair + c] for c in range(pair) for _ in range(G)])
        reach = stack([hor_recv[mate * pair + c] for c in range(pair) for _ in range(G)])
        rate = -1.0 / reach
        local = group * LANES + lane
        valid = (mine * L + local < length).astype(F32)
        step = 16
        near = [jnp.where(lane < LANES - k, jnp.exp(rate * (k - 1)), 0.0) for k in range(1, step + 1)]
        far = [jnp.where(lane < LANES - k, jnp.exp(rate * k), 0.0) for k in range(step, LANES, step)]
        lead_in = jnp.exp(rate * lane.astype(F32))
        hops = [1 << i for i in range(max(G - 1, 0).bit_length())]
        row_decay = [jnp.where(group + k < G, jnp.exp(rate * (k * LANES)), 0.0) for k in hops]
        into = jnp.where(group < G - 1, jnp.exp(rate * (LANES - 1 - lane).astype(F32)), 0.0)
        power = jnp.exp(rate * (L - 1 - local).astype(F32))
        decay = jnp.exp(rate)
        gains = stack([rw_recv[c * per + h] for c in range(pair) for h in range(per)])

        rbuf[s * pair + side] = part[mine]
        bytes_of(rbuf.at[pl.ds(0, n * pair - 1)], part_rs).wait()
        projected, squares = [], []
        for c in range(pair):
            for j in range(subs):
                first, second = rbuf[c, j, 0], rbuf[c, j, 1]
                for k in range(1, n):
                    first = first + rbuf[k * pair + c, j, 0]
                    second = second + rbuf[k * pair + c, j, 1]
                projected.append(first)
                squares.append(second)
        values = stack(projected) * lax.rsqrt(stack(squares) / total + EPS)
        held = values * valid
        change = (gains - values) * valid
        mixed = decay * change + held
        start = jnp.sum(lead_in * mixed, 1, keepdims=True)
        terms = [factor * pltpu.roll(mixed if k < step else held, LANES - k, 1)
                 for k, factor in enumerate(near, 1)]
        while len(terms) > 1:
            terms = [sum(terms[i + 1:i + 2], terms[i]) for i in range(0, len(terms), 2)]
        gae = change + terms[0]
        terms = [factor * pltpu.roll(gae, LANES - k * step, 1) for k, factor in enumerate(far, 1)]
        while len(terms) > 1:
            terms = [sum(terms[i + 1:i + 2], terms[i]) for i in range(0, len(terms), 2)]
        gae = gae + terms[0]
        start = jnp.broadcast_to(start, gae.shape)
        if G > 1:
            for k, factor in zip(hops, row_decay):
                start = start + factor * pltpu.roll(start, pair * rows - k * R, 0)
            gae = gae + into * pltpu.roll(start, pair * rows - R, 0)
        sums = jnp.where(lane == 1, jnp.sum(gae, 1, keepdims=True), 0.0)
        sums = jnp.where(lane == 2, 2.0 * jnp.sum(gae * power, 1, keepdims=True), sums)
        sums = jnp.where(lane == 3, jnp.sum(gae * gae, 1, keepdims=True), sums)
        sums = jnp.where((lane == 0) & (group == 0), start, sums)
        if G & (G - 1) == 0:
            for k in hops:
                sums = sums + pltpu.roll(sums, pair * rows - k * R, 0)
            for c in range(pair):
                sum_send[c * R:(c + 1) * R, :] = sums[c * rows:c * rows + R]
        else:
            for c in range(pair):
                summary = sums[c * rows:c * rows + R]
                for g in range(1, G):
                    summary = summary + sums[c * rows + g * R:c * rows + (g + 1) * R]
                sum_send[c * R:(c + 1) * R, :] = summary
        sum_recv[mine * pairs + mate] = sum_send[...]
        each_sum()
        for g in range(G):
            for c in range(pair):
                at = c * rows + g * R
                tok_send[g, 0, c * R:(c + 1) * R, :] = gae[at:at + R]
                tok_send[g, 1, c * R:(c + 1) * R, :] = values[at:at + R]
        for h in range(per):
            for j in range(nb):
                if j % pair != pair - 1:
                    tok_copy(h, j).start()
                else:
                    @pl.when((mine * per + h != s) | (j != b))
                    def _():
                        tok_copy(h, j).start()

                    @pl.when((mine * per + h == s) & (j == b))
                    def _():
                        tok_recv[mate] = tok_send[h * gb + (j * width) // LANES]

    spots = LANES // width
    spot = b % spots

    def pick(x):
        result = x[:, 0:width]
        for j in range(1, spots):
            result = jnp.where(spot == j, x[:, j * width:(j + 1) * width], result)
        return result

    every = nb * R
    lane = lax.broadcasted_iota(jnp.int32, (every, LANES), 1)
    local = (half * gb + (b * width) // LANES) * LANES + lane
    length = stack([len_recv[c] for c in range(nb)])
    rate = -1.0 / stack([hor_recv[c] for c in range(nb)])
    count = jnp.sum(jnp.minimum(length, T).astype(F32), 0, keepdims=True)
    share = 1.0 / count
    jump = jnp.exp(rate * float(L))
    power_out = pick(jnp.exp(rate * (L - 1 - local).astype(F32)))
    valid_out = pick((out_o * L + local < length).astype(F32))
    power = [jnp.exp(rate * (L - 1 - g * LANES - lane).astype(F32)) for g in range(G)]
    power_sum = jnp.broadcast_to(jnp.sum(sum(power[1:], power[0]), 1, keepdims=True), (every, LANES))
    power = [x * x for x in power]
    power_squares = jnp.broadcast_to(jnp.sum(sum(power[1:], power[0]), 1, keepdims=True), (every, LANES))

    part_rows = 2 * rows * (owners - 1) + info_rows
    sum_rows = Q * owners * pairs
    tok_rows = 2 * Q * pairs

    @pl.when(jnp.logical_not(is_owner))
    def _():
        wait_rows(part_rows + 2 * rows + gb * R, sent)
        wait_rows(sum_rows + tok_rows, late)

    @pl.when(own_rw)
    def _():
        wait_rows(part_rows + Q * (n * nb - 1) + 2 * Q * (per * nb - 1), sent)
        wait_rows(sum_rows - Q + tok_rows - 2 * Q, late)

    @pl.when(is_owner & jnp.logical_not(own_rw))
    def _():
        wait_rows(part_rows + gb * R + Q * (n * nb - 1) + 2 * Q * per * nb, sent)
        wait_rows(sum_rows - Q + tok_rows, late)

    gae = pick(stack([tok_recv[c, 0] for c in range(pairs)]))
    values = pick(stack([tok_recv[c, 1] for c in range(pairs)]))
    messages = [stack([sum_recv[o * pairs + c] for c in range(pairs)]) for o in range(owners)]

    def spread(o, i):
        return jnp.broadcast_to(messages[o][:, i:i + 1], (every, LANES))

    u = spread(owners - 1, 0)
    first = sum([spread(o, 1) for o in range(1, owners)], spread(0, 1))
    second = sum([spread(o, 3) for o in range(1, owners)], spread(0, 3))
    entering = jnp.zeros((every, LANES), F32)
    for o in reversed(range(owners - 1)):
        first = first + u * power_sum
        second = second + u * (spread(o, 2) + u * power_squares)
        entering = jnp.where(out_o == o, u, entering)
        if o:
            u = spread(o, 0) + jump * u
    mean = jnp.sum(first, 0, keepdims=True) * share
    var = jnp.maximum(jnp.sum(second, 0, keepdims=True) * share - mean * mean, 1.0)
    scale = lax.rsqrt(var)
    gae = gae + power_out * entering[:, 0:width]
    out_ref[every:2 * every, :] = (gae + values) * valid_out
    out_ref[0:every, :] = (gae - mean[:, 0:width]) * valid_out * scale[:, 0:width]


def per_device(hidden, gain, weight, rewards, mask, lengths, horizon):
    n = lax.axis_size("seq")
    nb = lax.axis_size("batch")
    pair = 2 - nb % 2
    owners = n // 2 if n % 4 == 0 else n
    R, T, depth = hidden.shape
    subs = max(T // owners // TILE, 1)
    chunks = owners * subs
    stream = R == 2 and depth == 2 * TILE and T == chunks * TILE
    block = rewards.shape[1]
    per = n // owners
    G = T // owners // LANES
    gb = block // LANES
    rows = G * R
    Q = pair * R
    pairs = nb // pair
    dma = pltpu.SemaphoreType.DMA
    both = pl.pallas_call(
        functools.partial(kernel, n, nb, pair, owners, subs, stream),
        out_shape=pltpu.VMEM((2 * R * nb, block // nb), F32),
        in_specs=[pl.BlockSpec(memory_space=pl.ANY)] * 7,
        out_specs=pl.BlockSpec(memory_space=pltpu.VMEM),
        scratch_shapes=[
            pltpu.VMEM((R, T, depth), jnp.bfloat16),
            pltpu.VMEM((depth,), F32),
            pltpu.VMEM((depth,), F32),
            pltpu.VMEM((R, block), F32),
            pltpu.VMEM((R, block), jnp.int32),
            pltpu.SMEM((R,), jnp.int32),
            pltpu.SMEM((R,), F32),
            pltpu.VMEM((owners, subs, 2, rows // subs, LANES), F32),
            pltpu.VMEM((n * pair, subs, 2, rows // subs, LANES), F32),
            pltpu.VMEM((gb * R, LANES), F32),
            pltpu.VMEM((pair * per, gb * R, LANES), F32),
            pltpu.VMEM((R, LANES), jnp.int32),
            pltpu.VMEM((nb, R, LANES), jnp.int32),
            pltpu.VMEM((R, LANES), F32),
            pltpu.VMEM((nb, R, LANES), F32),
            pltpu.VMEM((Q, LANES), F32),
            pltpu.VMEM((owners * pairs, Q, LANES), F32),
            pltpu.VMEM((G, 2, Q, LANES), F32),
            pltpu.VMEM((pairs, 2, Q, LANES), F32),
            pltpu.VMEM((2 * depth,), F32),
            pltpu.VMEM((2 * R, block), F32),
            pltpu.VMEM((2 * owners * rows + 2 * R * nb + Q * n * nb + 2 * Q * per * nb + rows, LANES), F32),
            pltpu.VMEM((2, R, TILE, LANES), F32),
            dma((chunks,)), dma((4,)), dma(()), dma(()), dma(()), dma(()),
        ],
        compiler_params=pltpu.CompilerParams(collective_id=0, has_side_effects=True),
    )(hidden, gain, weight, rewards, mask, lengths, horizon)
    return both[:R * nb], both[R * nb:]


def solution(mesh):
    return jax.shard_map(
        per_device,
        mesh=mesh,
        in_specs=(
            P("batch", None, "seq"),
            P("seq"),
            P("seq"),
            P("batch", "seq"),
            P("batch", "seq"),
            P("batch"),
            P("batch"),
        ),
        out_specs=(P(None, ("seq", "batch")), P(None, ("seq", "batch"))),
        check_vma=False,
    )
```

time: 14.7 us -> 14.4 us (0.980)
  Pallas kernels: 13.3 us -> 13.1 us
    pallas_call x1, Pallas kernels: 13.3 us -> 13.1 us  [per_device(): pl.pallas_call(functools.partial(kernel, n, nb, pair, owners, subs, strea...]
where the time goes in v4:
time: 14.4 us; the launch traced here: 14.3 us
  Pallas kernels  13.1 us (91%)
  between operations  0.64 us (4%)
  local copies, waits for them, and re-layouts  0.6 us (4%)
    pallas_call x1, Pallas kernels, per_device(): pl.pallas_call(functools.partial(kernel, n, nb, pair, owners, subs, strea...  13.1 us
    slice x1, local copies, waits for them, and re-layouts, per_device(): return (both[:R * nb], both[R * nb:])  0.6 us

profile of v4, /device:TPU:0, one launch (start us, length us, event | category | flops | bytes accessed | tf_op | source)
XLA Modules:
  0.0 14.3 jit_solution(10136221795235042516)
XLA Ops:
  0.6 13.1 %shard_map.86 = f32[16,64]{1,0:T(8,128)S(1)} custom-call(bf16[2,2048,512]{2,1,0:T(8,128)(2,1)} %hidden.1, f32[512]{0:T(512)} %gain.1, f32[512]{0:T(512)} %weight.1, f32[2,256]{1,0:T(2,128)} %rewards.1, s32[2,256]{1,0:T(2,128)} %mask.1, s32[2]{0:T(128)} %lengths.1, f32[2]{0:T(128)} %horizon.1), custom_call_target="tpu_custom_call" | custom-call | tf_op jit(solution)/shard_map/pallas_call | solution.py:452
  13.7 0.6 %fusion = (f32[8,64]{1,0:T(8,128)}, f32[8,64]{1,0:T(8,128)}) fusion(f32[16,64]{1,0:T(8,128)S(1)} %shard_map.86), kind=kLoop, calls=%fused_computation | loop fusion | bytes 8192 | tf_op jit(solution)/shard_map/slice | solution.py:485

commit v5 on v4

--- a/solution.py
+++ b/solution.py
@@ -62,24 +62,26 @@
             return (s + back) % owners
         return (near_high + back // 2) % (owners // 2) * 2 + (near_low + back) % 2
 
-    def chunk_copy(c):
+    plan = [(c, tuple(range(R))) for c in range(owners * subs)]
+
+    def chunk_copy(c, rs, i):
         span = pl.ds(turn(c // subs) * L + c % subs * S, S)
-        return pltpu.make_async_copy(hidden.at[:, span, :], hv.at[:, span, :], chunk_sem.at[c])
+        at = slice(None) if len(rs) == R else rs[0]
+        return pltpu.make_async_copy(hidden.at[at, span, :], hv.at[at, span, :], chunk_sem.at[i])
 
     def wait_rows(count, sem):
         if count:
             bytes_of(any_rows.at[pl.ds(0, count)], sem).wait()
 
-    pltpu.make_async_copy(gain, gain_v, small_sem.at[0]).start()
-    pltpu.make_async_copy(weight, weight_v, small_sem.at[0]).start()
-    for c in range(owners * subs):
-        chunk_copy(c).start()
-    pltpu.make_async_copy(rewards, rew_v, small_sem.at[1]).start()
-    pltpu.make_async_copy(mask, mask_v, small_sem.at[1]).start()
-    ends = [pltpu.make_async_copy(lengths, len_s, small_sem.at[2]),
-            pltpu.make_async_copy(horizon, hor_s, small_sem.at[3])]
-    for copy in ends:
-        copy.start()
+    smalls = [
+        pltpu.make_async_copy(src, dst, small_sem.at[i])
+        for i, src, dst in ((0, gain, gain_v), (0, weight, weight_v), (1, rewards, rew_v),
+                            (1, mask, mask_v), (2, lengths, len_s), (3, horizon, hor_s))]
+    for i, (c, rs) in enumerate(plan):
+        chunk_copy(c, rs, i).start(priority=int(i > 1))
+        if i == 0:
+            for copy in smalls:
+                copy.start()
     barrier = pltpu.get_barrier_semaphore()
     for k in range(1, nb):
         pl.semaphore_signal(barrier, inc=1, device_id={"batch": lax.rem(b + k, nb)},
@@ -128,18 +130,20 @@
         def _():
             part_copy(o, j).start()
 
-    meet = min(2, owners * subs - 1)
+    meet = min(1, owners * subs - 1)
+
+    pieces = head_pieces()
+    bytes_of(both_m, small_sem.at[1]).wait()
+    for copy in smalls[4:]:
+        copy.wait()
+    rw = rew_v[...] * mask_v[...].astype(F32)
+    for g in range(gb):
+        rw_send[g * R:(g + 1) * R, :] = rw[:, g * LANES:(g + 1) * LANES]
+    for r in range(R):
+        len_send[r:r + 1, :] = jnp.full((1, LANES), len_s[r], jnp.int32)
+        hor_send[r:r + 1, :] = jnp.full((1, LANES), hor_s[r], F32)
 
     def enter():
-        bytes_of(both_m, small_sem.at[1]).wait()
-        for copy in ends:
-            copy.wait()
-        rw = rew_v[...] * mask_v[...].astype(F32)
-        for g in range(gb):
-            rw_send[g * R:(g + 1) * R, :] = rw[:, g * LANES:(g + 1) * LANES]
-        for r in range(R):
-            len_send[r:r + 1, :] = jnp.full((1, LANES), len_s[r], jnp.int32)
-            hor_send[r:r + 1, :] = jnp.full((1, LANES), hor_s[r], F32)
         met = jnp.where(is_owner, owners - 1, owners) + nb - 1
         pl.semaphore_wait(barrier, met)
 
@@ -158,10 +162,10 @@
             squares = squares + wide * wide
         return squares
 
-    def compute(k, pieces):
+    def compute(k, carry):
         o = turn(k)
         for j in range(subs):
-            chunk_copy(k * subs + j).wait()
+            chunk_copy(k * subs + j, range(R), k * subs + j).wait()
         for g in range(G):
             for r in range(R):
                 at = pl.ds(pl.multiple_of(o * L + g * LANES, LANES), LANES)
@@ -178,38 +182,30 @@
 
         for j in range(subs):
             send_part(o, j)
-        return pieces
+        return carry
 
     def streamed(*accs):
         for acc in accs:
             pltpu.matmul_pop(acc)
-        pieces = None
-        units = [(r, m) for r in range(R) for m in range(2)]
-        for step in range(owners * subs + 1):
-            if step < owners * subs:
-                o, j = turn(step // subs), step % subs
-                chunk_copy(step).wait()
-                blocks = [hv[r, pl.ds(pl.multiple_of(o * L + j * S, S), S), :] for r in range(R)]
-                if step == 0:
-                    for r, m in units:
-                        pltpu.matmul_push_rhs(blocks[r][:, m * TILE:(m + 1) * TILE],
-                                              staging_register=r, mxu_index=m, transpose=True)
-                    for r in range(R):
-                        held_squares[step % 2, r] = squares_of(blocks[r])
-                    pieces = head_pieces()
-                for r, m in units:
-                    if step:
-                        pltpu.matmul_push_rhs(blocks[r][:, m * TILE:(m + 1) * TILE],
-                                              staging_register=r, mxu_index=m, transpose=True)
-                    pltpu.matmul_acc_lhs(accs[(step % 2 * R + r) * 2 + m],
-                                         pieces[:, m * TILE:(m + 1) * TILE], load_staged_rhs=r)
-                if step:
-                    for r in range(R):
-                        held_squares[step % 2, r] = squares_of(blocks[r])
+        for step in range(len(plan) + 1):
+            if step < len(plan):
+                c, rs = plan[step]
+                o, j = turn(c // subs), c % subs
+                chunk_copy(c, rs, step).wait()
+                for r in rs:
+                    h = hv[r, pl.ds(pl.multiple_of(o * L + j * S, S), S), :]
+                    for m in range(2):
+                        cols = slice(m * TILE, (m + 1) * TILE)
+                        pltpu.matmul_push_rhs(h[:, cols], staging_register=r, mxu_index=m,
+                                              transpose=True)
+                        pltpu.matmul_acc_lhs(accs[(step % 2 * R + r) * 2 + m], pieces[:, cols],
+                                             load_staged_rhs=r)
+                    held_squares[step % 2, r] = squares_of(h)
             if step:
                 last = step - 1
-                o, j = turn(last // subs), last % subs
-                for r in range(R):
+                c, rs = plan[last]
+                o, j = turn(c // subs), c % subs
+                for r in rs:
                     at = (last % 2 * R + r) * 2
                     sums = pltpu.matmul_pop(accs[at]) + pltpu.matmul_pop(accs[at + 1])
                     sums = jnp.sum(sums[0:8], 0, keepdims=True)
@@ -220,13 +216,15 @@
                         part[o, j, 1, row:row + 1, :] = jnp.sum(square.T, 0, keepdims=True)
                 if last == meet:
                     enter()
-                for c in range(last if last > meet else 0, last + 1 if last >= meet else 0):
-                    send_part(turn(c // subs), c % subs)
+                    for i in range(c):
+                        send_part(turn(i // subs), i % subs)
+                if last >= meet and rs[-1] == R - 1:
+                    send_part(o, j)
 
     if stream:
         pl.run_scoped(streamed, *[pltpu.ACC(i % 2)((16, TILE), F32) for i in range(4 * R)])
     else:
-        lax.fori_loop(0, owners, compute, head_pieces())
+        lax.fori_loop(0, owners, compute, 0)
 
     @pl.when(own_rw)
     def _():
@@ -368,9 +366,9 @@
     spot = b % spots
 
     def pick(x):
-        result = x[:, 0:width]
+        result = x
         for j in range(1, spots):
-            result = jnp.where(spot == j, x[:, j * width:(j + 1) * width], result)
+            result = jnp.where(spot == j, pltpu.roll(x, LANES - j * width, 1), result)
         return result
 
     every = nb * R
@@ -427,9 +425,9 @@
     mean = jnp.sum(first, 0, keepdims=True) * share
     var = jnp.maximum(jnp.sum(second, 0, keepdims=True) * share - mean * mean, 1.0)
     scale = lax.rsqrt(var)
-    gae = gae + power_out * entering[:, 0:width]
-    out_ref[every:2 * every, :] = (gae + values) * valid_out
-    out_ref[0:every, :] = (gae - mean[:, 0:width]) * valid_out * scale[:, 0:width]
+    gae = gae + power_out * entering
+    out_ref[every:2 * every, :] = ((gae + values) * valid_out)[:, 0:width]
+    out_ref[0:every, :] = ((gae - mean) * valid_out * scale)[:, 0:width]
 
 
 def per_device(hidden, gain, weight, rewards, mask, lengths, horizon):

time: 14.4 us -> 14.3 us (level)
  Pallas kernels: 13.1 us -> 12.9 us
    pallas_call x1, Pallas kernels: 13.1 us -> 12.9 us  [per_device(): pl.pallas_call(functools.partial(kernel, n, nb, pair, owners, subs, strea...]
where the time goes in v5:
time: 14.3 us; the launch traced here: 14.1 us
  Pallas kernels  12.9 us (90%)
  between operations  0.64 us (4%)
  local copies, waits for them, and re-layouts  0.6 us (4%)
    pallas_call x1, Pallas kernels, per_device(): pl.pallas_call(functools.partial(kernel, n, nb, pair, owners, subs, strea...  12.9 us
    slice x1, local copies, waits for them, and re-layouts, per_device(): return (both[:R * nb], both[R * nb:])  0.6 us

profile of v5, /device:TPU:0, one launch (start us, length us, event | category | flops | bytes accessed | tf_op | source)
XLA Modules:
  0.0 14.1 jit_solution(3146331218575555264)
XLA Ops:
  0.6 12.9 %shard_map.86 = f32[16,64]{1,0:T(8,128)S(1)} custom-call(bf16[2,2048,512]{2,1,0:T(8,128)(2,1)} %hidden.1, f32[512]{0:T(512)} %gain.1, f32[512]{0:T(512)} %weight.1, f32[2,256]{1,0:T(2,128)} %rewards.1, s32[2,256]{1,0:T(2,128)} %mask.1, s32[2]{0:T(128)} %lengths.1, f32[2]{0:T(128)} %horizon.1), custom_call_target="tpu_custom_call" | custom-call | tf_op jit(solution)/shard_map/pallas_call | solution.py:450
  13.5 0.6 %fusion = (f32[8,64]{1,0:T(8,128)}, f32[8,64]{1,0:T(8,128)}) fusion(f32[16,64]{1,0:T(8,128)S(1)} %shard_map.86), kind=kLoop, calls=%fused_computation | loop fusion | bytes 8192 | tf_op jit(solution)/shard_map/slice | solution.py:483

commit v6 on v5

--- a/solution.py
+++ b/solution.py
@@ -62,12 +62,9 @@
             return (s + back) % owners
         return (near_high + back // 2) % (owners // 2) * 2 + (near_low + back) % 2
 
-    plan = [(c, tuple(range(R))) for c in range(owners * subs)]
-
-    def chunk_copy(c, rs, i):
+    def chunk_copy(c, r=slice(None)):
         span = pl.ds(turn(c // subs) * L + c % subs * S, S)
-        at = slice(None) if len(rs) == R else rs[0]
-        return pltpu.make_async_copy(hidden.at[at, span, :], hv.at[at, span, :], chunk_sem.at[i])
+        return pltpu.make_async_copy(hidden.at[r, span, :], hv.at[r, span, :], chunk_sem.at[c])
 
     def wait_rows(count, sem):
         if count:
@@ -77,9 +74,10 @@
         pltpu.make_async_copy(src, dst, small_sem.at[i])
         for i, src, dst in ((0, gain, gain_v), (0, weight, weight_v), (1, rewards, rew_v),
                             (1, mask, mask_v), (2, lengths, len_s), (3, horizon, hor_s))]
-    for i, (c, rs) in enumerate(plan):
-        chunk_copy(c, rs, i).start(priority=int(i > 1))
-        if i == 0:
+    for c in range(owners * subs):
+        for r in range(R):
+            chunk_copy(c, r).start(priority=int(c > 0))
+        if c == 0:
             for copy in smalls:
                 copy.start()
     barrier = pltpu.get_barrier_semaphore()
@@ -129,8 +127,6 @@
         @pl.when(jnp.logical_not(is_owner & (mine == o)))
         def _():
             part_copy(o, j).start()
-
-    meet = min(1, owners * subs - 1)
 
     pieces = head_pieces()
     bytes_of(both_m, small_sem.at[1]).wait()
@@ -165,7 +161,7 @@
     def compute(k, carry):
         o = turn(k)
         for j in range(subs):
-            chunk_copy(k * subs + j, range(R), k * subs + j).wait()
+            chunk_copy(k * subs + j).wait()
         for g in range(G):
             for r in range(R):
                 at = pl.ds(pl.multiple_of(o * L + g * LANES, LANES), LANES)
@@ -187,12 +183,11 @@
     def streamed(*accs):
         for acc in accs:
             pltpu.matmul_pop(acc)
-        for step in range(len(plan) + 1):
-            if step < len(plan):
-                c, rs = plan[step]
-                o, j = turn(c // subs), c % subs
-                chunk_copy(c, rs, step).wait()
-                for r in rs:
+        for step in range(owners * subs + 1):
+            if step < owners * subs:
+                o, j = turn(step // subs), step % subs
+                chunk_copy(step).wait()
+                for r in range(R):
                     h = hv[r, pl.ds(pl.multiple_of(o * L + j * S, S), S), :]
                     for m in range(2):
                         cols = slice(m * TILE, (m + 1) * TILE)
@@ -201,11 +196,12 @@
                         pltpu.matmul_acc_lhs(accs[(step % 2 * R + r) * 2 + m], pieces[:, cols],
                                              load_staged_rhs=r)
                     held_squares[step % 2, r] = squares_of(h)
-            if step:
+            if step == 0:
+                enter()
+            else:
                 last = step - 1
-                c, rs = plan[last]
-                o, j = turn(c // subs), c % subs
-                for r in rs:
+                o, j = turn(last // subs), last % subs
+                for r in range(R):
                     at = (last % 2 * R + r) * 2
                     sums = pltpu.matmul_pop(accs[at]) + pltpu.matmul_pop(accs[at + 1])
                     sums = jnp.sum(sums[0:8], 0, keepdims=True)
@@ -214,12 +210,7 @@
                         square = held_squares[last % 2, r, g * LANES:(g + 1) * LANES, :]
                         part[o, j, 0, row:row + 1, :] = sums[:, g * LANES:(g + 1) * LANES]
                         part[o, j, 1, row:row + 1, :] = jnp.sum(square.T, 0, keepdims=True)
-                if last == meet:
-                    enter()
-                    for i in range(c):
-                        send_part(turn(i // subs), i % subs)
-                if last >= meet and rs[-1] == R - 1:
-                    send_part(o, j)
+                send_part(o, j)
 
     if stream:
         pl.run_scoped(streamed, *[pltpu.ACC(i % 2)((16, TILE), F32) for i in range(4 * R)])

time: 14.3 us -> 14.2 us (level)
  no operation moved by 1% of the time
where the time goes in v6:
time: 14.2 us; the launch traced here: 14.1 us
  Pallas kernels  12.9 us (91%)
  between operations  0.64 us (5%)
  local copies, waits for them, and re-layouts  0.6 us (4%)
    pallas_call x1, Pallas kernels, per_device(): pl.pallas_call(functools.partial(kernel, n, nb, pair, owners, subs, strea...  12.9 us
    slice x1, local copies, waits for them, and re-layouts, per_device(): return (both[:R * nb], both[R * nb:])  0.6 us

profile of v6, /device:TPU:0, one launch (start us, length us, event | category | flops | bytes accessed | tf_op | source)
XLA Modules:
  0.0 14.1 jit_solution(16513375990058767526)
XLA Ops:
  0.6 12.9 %shard_map.86 = f32[16,64]{1,0:T(8,128)S(1)} custom-call(bf16[2,2048,512]{2,1,0:T(8,128)(2,1)} %hidden.1, f32[512]{0:T(512)} %gain.1, f32[512]{0:T(512)} %weight.1, f32[2,256]{1,0:T(2,128)} %rewards.1, s32[2,256]{1,0:T(2,128)} %mask.1, s32[2]{0:T(128)} %lengths.1, f32[2]{0:T(128)} %horizon.1), custom_call_target="tpu_custom_call" | custom-call | tf_op jit(solution)/shard_map/pallas_call | solution.py:441
  13.5 0.6 %fusion = (f32[8,64]{1,0:T(8,128)}, f32[8,64]{1,0:T(8,128)}) fusion(f32[16,64]{1,0:T(8,128)S(1)} %shard_map.86), kind=kLoop, calls=%fused_computation | loop fusion | bytes 8192 | tf_op jit(solution)/shard_map/slice | solution.py:474
